TPU v7x, 128 devices: a whole 4x4x4 slice. The times are simulated.
128 devices in a mesh: dp: 8 (over x, core), expert: 16 (over y, z).
Axes of the slice: x: 4, y: 4, z: 4, core: 2. Of those that a mesh axis runs over, the one named last changes fastest.
Arguments:
- grads: bfloat16 [131072, 4096], P(('dp', 'expert')), may hold values from -6 to 6
- block_expert: int32 [1024, 1], P(('dp', 'expert')), may hold values from 0 to 15; in each aligned block of 8 rows (0 to 7, 8 to 15, ...) at most 2 rows name the same one
- sketch: bfloat16 [16, 256, 4096], P('expert', None, 'dp'), may hold values from -0.09375 to 0.09375
Outputs:
- factor: bfloat16 [16, 256, 4096], P('expert')
Inputs may be any that keep to these rules, and one draw needn't show every extreme that they name: `block_expert`: among the 8 blocks of one device, at most 2 belong to one expert, and every expert has some block.
All inputs are finite; a program needn't handle non-finite values.
Results may differ from a plain program's by a relative error of at most 0.0031.
Values may be sent and summed in bfloat16 or wider, within the bound.
A program may use at most 256 MiB of HBM per device.

v0:
```python
import jax
import jax.numpy as jnp
from jax import lax
from jax.sharding import PartitionSpec as P

D = 4096
BLOCK = 128
CAP = 2
ITERS = 5


EPSILON = 1e-06


def in_blocks(x, dim, length):
    lengths = x.shape
    parts = x.reshape(*lengths[:dim], length, lengths[dim] // length, *lengths[dim + 1 :])
    return jnp.moveaxis(parts, dim, 0)


def cut_rows(length, count):
    turn = length // count
    if turn >= 8:
        turn -= turn % 8
    return [turn * k for k in range(1, count)]


def laid_out(parts, dim):
    parts = jnp.moveaxis(parts, 0, dim)
    lengths = parts.shape
    return parts.reshape(*lengths[:dim], lengths[dim] * lengths[dim + 1], *lengths[dim + 2 :])


def cut_exchange(x, axis, pieces, split_dim, concat_dim):
    parts = in_blocks(x, split_dim, lax.axis_size(axis))
    split_at = max(range(1, max(2, parts.ndim - 1)), key=lambda d: parts.shape[d])
    gathered = []
    for piece in jnp.split(parts, cut_rows(parts.shape[split_at], pieces), axis=split_at):
        if piece.size:
            gathered.append(lax.all_to_all(piece, axis, split_axis=0, concat_axis=0, tiled=True))
    return laid_out(jnp.concatenate(gathered, axis=split_at), concat_dim)


def newton_step(iterate, inner):
    return 1.5 * iterate - 0.5 * jnp.dot(inner, iterate, precision=lax.Precision.HIGHEST)


def shards(grads, block_expert, sketch):
    count_blocks = block_expert.shape[0]
    columns = grads.shape[1]
    experts = lax.axis_size("expert")
    replicas = lax.axis_size("dp")
    blocks = grads.reshape(count_blocks, BLOCK, columns)
    owners = block_expert[:, 0]
    same_owner = owners[None, :] == owners[:, None]
    earlier = lax.broadcasted_iota(
        jnp.int32, (count_blocks, count_blocks), 1
    ) < lax.broadcasted_iota(jnp.int32, (count_blocks, count_blocks), 0)
    places = jnp.sum((same_owner & earlier).astype(jnp.int32), axis=1)
    targets = owners * CAP + places
    outgoing = jnp.zeros((experts * CAP, BLOCK, columns), jnp.bfloat16).at[targets].set(blocks)
    outgoing = outgoing.reshape(experts, CAP * BLOCK, columns)
    incoming = cut_exchange(outgoing, "expert", 2, 0, 0)
    arrived = incoming.reshape(experts * CAP * BLOCK, columns)
    basis_full = lax.all_gather(sketch, "dp", axis=2, tiled=True)[0]
    projected = lax.dot_general(
        basis_full, arrived, (((1,), (1,)), ((), ())), preferred_element_type=jnp.float32
    ).astype(jnp.bfloat16)
    partial_term = jnp.dot(projected, arrived, preferred_element_type=jnp.float32)
    basis_gram = lax.dot_general(
        basis_full, basis_full, (((1,), (1,)), ((), ())), preferred_element_type=jnp.float32
    )
    average = float(BLOCK * count_blocks * replicas)
    gradient_term = lax.psum(partial_term, "dp")
    unscaled = (
        jnp.dot(basis_gram, basis_full.astype(jnp.float32), precision=lax.Precision.HIGHEST)
        + gradient_term / average
    )
    iterate = unscaled / jnp.sqrt(jnp.sum(unscaled * unscaled) + EPSILON)
    for step in range(ITERS):
        inner = lax.dot_general(
            iterate, iterate, (((1,), (1,)), ((), ())), precision=lax.Precision.HIGHEST
        )
        iterate = newton_step(iterate, inner)
    return (iterate * D**0.5).astype(jnp.bfloat16)[None]


def solution(mesh):
    in_specs = (P(("dp", "expert"), None), P(("dp", "expert"), None), P("expert", None, "dp"))
    out_specs = P("expert", None, None)
    return jax.shard_map(shards, mesh=mesh, in_specs=in_specs, out_specs=out_specs, check_vma=False)
```

profile of v0, /device:TPU:1, one launch (start us, length us, event | category | flops | bytes accessed | tf_op | source)
XLA Modules:
  0.0 776.8 jit_solution(16272449002042471784)
XLA Ops:
  6.5 0.9 convert_reduce_fusion
  7.4 0.7 fusion.16
  8.1 11.0 %broadcast_in_dim.7 = bf16[32,128,4096]{2,1,0:T(8,128)(2,1)} broadcast(bf16[]{:T(256)} %constant.10.clone.1), dimensions={} | broadcast | bytes 33554432 | tf_op jit(solution)/shard_map/broadcast_in_dim | solution.py:61
  19.1 21.4 %scatter_fusion = bf16[32,128,4096]{2,1,0:T(8,128)(2,1)} fusion(bf16[32,128,4096]{2,1,0:T(8,128)(2,1)} %broadcast_in_dim.7, s32[8]{0:T(128)S(1)} %fusion.16, bf16[8,128,4096]{2,1,0:T(8,128)(2,1)} %bitcast.44), kind=kCustom, calls=%fused_computation | custom fusion | bytes 25165856 | tf_op jit(solution)/shard_map/scatter | solution.py:61
  40.5 18.2 %fusion.17 = (bf16[16,1,128,4096]{3,2,1,0:T(8,128)(2,1)S(1)}, bf16[16,1,128,4096]{3,2,1,0:T(8,128)(2,1)}) fusion(bf16[16,1,256,4096]{3,2,1,0:T(8,128)(2,1)} %bitcast.42), kind=kLoop, calls=%fused_computation.31 | loop fusion | bytes 67108864 | tf_op jit(solution)/shard_map/split | solution.py:38
  58.6 194.5 %all_to_all.10 = bf16[16,1,128,4096]{3,2,1,0:T(8,128)(2,1)} all-to-all(bf16[16,1,128,4096]{3,2,1,0:T(8,128)(2,1)S(1)} %get-tuple-element.5), channel_id=1, replica_groups=mesh['dp'=8,'expert'=16] {'expert'}, dimensions={0} | all-to-all | bytes 33554432 | tf_op jit(solution)/shard_map/all_to_all | solution.py:40
  253.2 5.1 all-to-all-start.1
  258.3 0.0 all-gather.2.cloned.1.call-start
  258.4 0.7 all-gather.2.cloned.1.call-update
  259.0 0.0 all-reduce.2.cloned.1.call-start
  259.1 295.1 %all-to-all-done.1 = bf16[16,1,128,4096]{3,2,1,0:T(8,128)(2,1)} async-done(((bf16[16,1,128,4096]{3,2,1,0:T(8,128)(2,1)}), bf16[16,1,128,4096]{3,2,1,0:T(8,128)(2,1)}, u32[]{:S(2)}, u32[]{:S(2)}) %all-to-all-start.1) | async-done | bytes 16777248 | tf_op jit(solution)/shard_map/all_to_all | solution.py:40
  554.2 22.8 %pad_maximum_fusion = bf16[16,1,256,4096]{3,2,1,0:T(8,128)(2,1)} fusion(bf16[16,1,128,4096]{3,2,1,0:T(8,128)(2,1)} %all-to-all-done.1, bf16[16,1,128,4096]{3,2,1,0:T(8,128)(2,1)} %all_to_all.10), kind=kLoop, calls=%fused_computation.1 | loop fusion | flops 67108864 | bytes 67108864 | tf_op jit(solution)/shard_map/concatenate | solution.py:41
  577.0 0.0 all-gather.2.cloned.1.call-done
  577.0 47.4 %fusion.8 = f32[256,4096]{1,0:T(8,128)} fusion(bf16[4096,4096]{1,0:T(8,128)(2,1)} %bitcast.43, bf16[1,256,4096]{2,1,0:T(8,128)(2,1)} %all-gather.2.cloned.1.call-done), kind=kOutput, calls=%fused_computation.18 | convolution fusion | flops 17180917760 | bytes 39845888 | tf_op jit(solution)/shard_map/dot_general | solution.py:69
  624.4 0.0 copy-start.1
  624.4 0.0 all-reduce.2.cloned.1.call-update
  624.4 1.6 copy-done.1
  626.0 0.7 fusion.12
  626.7 75.7 %all-reduce.2.cloned.1.call-done = f32[256,4096]{1,0:T(8,128)} async-done(((f32[256,4096]{1,0:T(8,128)}), f32[256,4096]{1,0:T(8,128)}) %all-reduce.2.cloned.1.call-update) | async-done | bytes 4194320 | tf_op jit(solution)/shard_map/psum | solution.py:74
  702.4 7.3 multiply_reduce_fusion
  710.4 0.0 copy-start
  710.4 23.0 %fusion.14 = f32[256,256]{1,0:T(8,128)S(1)} fusion(f32[256,4096]{1,0:T(8,128)} %get-tuple-element.8, f32[]{:T(128)S(6)} %sqrt.3), kind=kOutput, calls=%fused_computation.24 | convolution fusion | flops 3222274048 | bytes 4456452 | tf_op jit(solution)/shard_map/dot_general | solution.py:81
  733.4 0.0 copy-done
  733.4 4.1 fusion.4
  737.5 3.5 fusion.18
  741.1 4.1 fusion.3
  745.2 3.9 fusion.19
  749.1 4.1 fusion.2
  753.3 3.5 fusion.20
  756.8 4.3 fusion.1
  761.1 3.5 fusion.21
  764.6 5.1 fusion.7
Async XLA Ops:
  253.2 301.0 %all-to-all-start.1 = ((bf16[16,1,128,4096]{3,2,1,0:T(8,128)(2,1)}), bf16[16,1,128,4096]{3,2,1,0:T(8,128)(2,1)}, u32[]{:S(2)}, u32[]{:S(2)}) async-start(bf16[16,1,128,4096]{3,2,1,0:T(8,128)(2,1)} %get-tuple-element.6), calls=%async_computation.1 | async-start | bytes 33554432 | tf_op jit(solution)/shard_map/all_to_all | solution.py:40
  258.3 318.7 %all-gather.2.cloned.1.call-start = ((), (), s32[]{:S(2)}) async-start(), calls=%async_computation.2 | async-start | bytes 2359296 | tf_op jit(solution)/shard_map/all_gather | solution.py:65
  259.0 443.4 %all-reduce.2.cloned.1.call-start = ((), (), s32[]{:S(2)}) async-start(), calls=%async_computation.3 | async-start | bytes 8388608 | tf_op jit(solution)/shard_map/psum | solution.py:74
  624.4 1.6 copy-start.1
  710.4 23.0 %copy-start = (f32[256,4096]{1,0:T(8,128)S(1)}, f32[256,4096]{1,0:T(8,128)}, u32[]{:S(2)}) copy-start(f32[256,4096]{1,0:T(8,128)} %get-tuple-element.8) | copy-start | bytes 12582916
Sparse Core Ops, SparseCore 0:
  260.8 28.8 all-gather.1
  624.5 77.8 all-reduce.1
where the time goes:
time: 782 us; the launch traced here: 777 us
  waiting for transfers between devices  372 us (48%)
  blocking collectives  195 us (25%)
  matrix products  115 us (15%)
  local copies, waits for them, and re-layouts  52.1 us (7%)
  other arithmetic  24.4 us (3%)
  between operations  14.4 us (2%)
    all_to_all x1, waiting for transfers between devices, cut_exchange(): lax.all_to_all(piece, axis, split_axis=0, concat_axis=0, tiled=True)  295 us
    all_to_all x1, blocking collectives, cut_exchange(): lax.all_to_all(piece, axis, split_axis=0, concat_axis=0, tiled=True)  195 us
    psum x1, waiting for transfers between devices, shards(): gradient_term = lax.psum(partial_term, 'dp')  75.7 us
    dot_general x1, matrix products, shards(): jnp.dot(projected, arrived, preferred_element_type=jnp.float32)  47.4 us
    dot_general x5, matrix products, shards(): lax.dot_general(iterate, iterate, (((1,), (1,)), ((), ())), precision=lax...  37.5 us
    concatenate x1, other arithmetic, cut_exchange(): return laid_out(jnp.concatenate(gathered, axis=split_at), concat_dim)  22.8 us
    dot_general x5, matrix products, newton_step(): jnp.dot(inner, iterate, precision=lax.Precision.HIGHEST)  21.7 us
    scatter x1, local copies, waits for them, and re-layouts, shards(): jnp.zeros((experts * CAP, BLOCK, columns), jnp.bfloat16).at[targets]  21.4 us
  transfers between devices with their start and end apart: 3, of which 2 were waited for; matrix products, arithmetic and copies ran while one was open for 3% of the time, Pallas kernels for 0%

commit v1 on v0

v1 whole, which is shorter than its diff:
```python
import functools

import jax
import jax.numpy as jnp
from jax import lax
from jax.experimental import pallas as pl
from jax.experimental.pallas import tpu as pltpu
from jax.sharding import PartitionSpec as P

D = 4096
L = 256
BLOCK = 128
NBLK = 8
EXPERTS = 16
ITERS = 5
N_DP = 8
COLS = D // N_DP
QUARTER = D // 4
HALF = L // 2
EPSILON = 1e-06
HIGHEST = lax.Precision.HIGHEST
MESH = pl.DeviceIdType.MESH
RING = 4
PARTS = ((0, 48), (48, 48), (96, 32))
ORDERS = ((0, 1, 2), (1, 2, 0), (2, 0, 1))


def mm_nt(a, b):
    return lax.dot_general(a, b, (((1,), (1,)), ((), ())), preferred_element_type=jnp.float32)


def position():
    dp, expert = lax.axis_index("dp"), lax.axis_index("expert")
    return (dp // 2, expert // 4, lax.rem(expert, 4)), lax.rem(dp, 2)


def device(coords, core):
    return (2 * coords[0] + core, 4 * coords[1] + coords[2])


def moved(coords, axis, by):
    return tuple(lax.rem(c + by, RING) if k == axis else c for k, c in enumerate(coords))


def meet(coords, core):
    barrier = pltpu.get_barrier_semaphore()
    peers = [device(moved(coords, a, by), core) for a in range(3) for by in (1, 3)]
    peers.append(device(coords, 1 - core))
    for peer in peers:
        pl.semaphore_signal(barrier, inc=1, device_id=peer, device_id_type=MESH)
    pl.semaphore_wait(barrier, len(peers))


def gather_kernel(sketch_ref, grads_ref, basis_ref, other_ref, send, recv, pair_send, pair_recv, local):
    coords, core = position()
    meet(coords, core)
    partner = device(coords, 1 - core)
    mine = tuple(pl.ds(c, 1) for c in coords)
    cols = pl.ds(pl.multiple_of(core * COLS, COLS), COLS)
    own_rows = pl.ds(pl.multiple_of(core * HALF, HALF), HALF)
    other_rows = pl.ds(pl.multiple_of((1 - core) * HALF, HALF), HALF)
    spot = basis_ref.at[coords[0], coords[1], coords[2], :, cols]
    keep = pltpu.make_async_copy(sketch_ref.at[own_rows], spot, local)
    keep.start()
    give = pltpu.make_async_remote_copy(
        sketch_ref.at[other_rows], spot, pair_send.at[0], pair_recv.at[0], partner, MESH
    )
    give.start()
    swap = pltpu.make_async_remote_copy(
        grads_ref, other_ref, pair_send.at[1], pair_recv.at[1], partner, MESH
    )
    swap.start()
    keep.wait()
    give.wait()

    def view(part, phase, shift, half):
        first, count = PARTS[part]
        order = ORDERS[part]
        index = list(mine)
        for axis in order[:phase]:
            index[axis] = slice(None)
        axis = order[phase]
        index[axis] = pl.ds(lax.rem(coords[axis] + shift, RING), 1)
        columns = slice(None) if half is None else pl.ds(half * (QUARTER // 2), QUARTER // 2)
        return basis_ref.at[index[0], index[1], index[2], pl.ds(first, count), columns]

    def copy(part, phase, which, shift, half, by):
        ref = view(part, phase, shift, half)
        return pltpu.make_async_remote_copy(
            ref,
            ref,
            send.at[part, phase, which],
            recv.at[part, phase, which],
            device(moved(coords, ORDERS[part][phase], by), core),
            MESH,
        )

    def arrived(part, phase, which, shift, half):
        ref = view(part, phase, shift, half)
        pltpu.make_async_copy(ref, ref, recv.at[part, phase, which]).wait()

    sent = []

    def start(*args):
        c = copy(*args)
        c.start()
        sent.append(c)

    for part in range(3):
        start(part, 0, 0, 0, None, 1)
        start(part, 0, 1, 0, None, 3)
    for phase in range(3):
        for part in range(3):
            arrived(part, phase, 0, 3, None)
            start(part, phase, 2, 3, 0, 1)
            arrived(part, phase, 1, 1, None)
            start(part, phase, 3, 1, 1, 3)
        for part in range(3):
            arrived(part, phase, 2, 2, 0)
            arrived(part, phase, 3, 2, 1)
            if phase < 2:
                start(part, phase + 1, 0, 0, None, 1)
                start(part, phase + 1, 1, 0, None, 3)
    for c in sent:
        c.wait_send()
    swap.wait()


def gather(sketch, grads):
    return pl.pallas_call(
        gather_kernel,
        out_shape=(
            jax.ShapeDtypeStruct((4, 4, 4, HALF, QUARTER), jnp.bfloat16),
            jax.ShapeDtypeStruct(grads.shape, jnp.bfloat16),
        ),
        in_specs=[
            pl.BlockSpec(memory_space=pltpu.VMEM),
            pl.BlockSpec(memory_space=pl.ANY),
        ],
        out_specs=(pl.BlockSpec(memory_space=pl.ANY), pl.BlockSpec(memory_space=pl.ANY)),
        scratch_shapes=[
            pltpu.SemaphoreType.DMA((3, 3, 4)),
            pltpu.SemaphoreType.DMA((3, 3, 4)),
            pltpu.SemaphoreType.DMA((2,)),
            pltpu.SemaphoreType.DMA((2,)),
            pltpu.SemaphoreType.DMA,
        ],
        compiler_params=pltpu.CompilerParams(collective_id=0, has_side_effects=True),
    )(sketch, grads)


def term_kernel(count_ref, slot_ref, own_ref, other_ref, s_ref, t_ref, g_ref, p_ref, sem):
    e = pl.program_id(0)
    count = count_ref[e]
    rows_of = NBLK * BLOCK

    @pl.when(e == 0)
    def _():
        first = pltpu.make_async_copy(own_ref, g_ref.at[0:rows_of], sem.at[0])
        second = pltpu.make_async_copy(other_ref, g_ref.at[rows_of : 2 * rows_of], sem.at[1])
        first.start()
        second.start()
        first.wait()
        second.wait()

    def rows(j):
        return pl.ds(pl.multiple_of(slot_ref[4 * e + j] * BLOCK, BLOCK), BLOCK)

    def pair(k, lo, hi):
        return jnp.concatenate([g_ref[rows(2 * k), lo:hi], g_ref[rows(2 * k + 1), lo:hi]], axis=0)

    @pl.when(count == 0)
    def _():
        t_ref[...] = jnp.zeros_like(t_ref)

    for k in range(2):

        @pl.when(count > 2 * k)
        def _(k=k):
            acc = jnp.zeros((HALF, 2 * BLOCK), jnp.float32)
            for x in range(4):
                acc += mm_nt(s_ref[x, 0, 0], pair(k, x * QUARTER, (x + 1) * QUARTER))
            place = lax.broadcasted_iota(jnp.int32, acc.shape, 1) // BLOCK + 2 * k
            p_ref[k] = jnp.where(place < count, acc, 0.0).astype(jnp.bfloat16)

    def emit(pairs):
        for x in range(4):
            for h in range(2):
                lo = x * QUARTER + h * COLS
                total = None
                for k in range(pairs):
                    part = jnp.dot(p_ref[k], pair(k, lo, lo + COLS), preferred_element_type=jnp.float32)
                    total = part if total is None else total + part
                t_ref[x, 0, 0, :, h * COLS : (h + 1) * COLS] = total.astype(jnp.bfloat16)

    pl.when((count > 0) & (count <= 2))(functools.partial(emit, 1))
    pl.when(count > 2)(functools.partial(emit, 2))


def slot_table(owners):
    ids = jnp.arange(EXPERTS, dtype=jnp.int32)
    hit = owners[None, :] == ids[:, None]
    count = jnp.sum(hit.astype(jnp.int32), axis=1)
    blocks = owners.shape[0]
    b = jnp.arange(blocks, dtype=jnp.int32)
    rank = jnp.sum(hit[:, None, :] & (b[None, :] < b[:, None])[None], axis=2).astype(jnp.int32)
    slots = [
        jnp.sum(jnp.where(hit & (rank == j), b[None, :], 0), axis=1) for j in range(4)
    ]
    return count, jnp.stack(slots, axis=1).reshape(-1)


def local_terms(count, slots, basis, grads, other):
    spec = pl.BlockSpec((4, 1, 1, HALF, QUARTER), lambda e, *_: (0, e // 4, e % 4, 0, 0))
    grid_spec = pltpu.PrefetchScalarGridSpec(
        num_scalar_prefetch=2,
        grid=(EXPERTS,),
        in_specs=[pl.BlockSpec(memory_space=pl.ANY), pl.BlockSpec(memory_space=pl.ANY), spec],
        out_specs=spec,
        scratch_shapes=[
            pltpu.VMEM((2 * NBLK * BLOCK, D), jnp.bfloat16),
            pltpu.VMEM((2, HALF, 2 * BLOCK), jnp.bfloat16),
            pltpu.SemaphoreType.DMA((2,)),
        ],
    )
    return pl.pallas_call(
        term_kernel,
        grid_spec=grid_spec,
        out_shape=jax.ShapeDtypeStruct(basis.shape, jnp.bfloat16),
        compiler_params=pltpu.CompilerParams(
            dimension_semantics=("arbitrary",), vmem_limit_bytes=48 * 1024 * 1024
        ),
        cost_estimate=pl.CostEstimate(
            flops=8 * NBLK * BLOCK * HALF * D, bytes_accessed=48 << 20, transcendentals=0
        ),
    )(count, slots, grads, other, basis)


def reduce_kernel(
    t_ref, out_ref, own0, own1, own2, far0, far1, far2, near0, near1, near2,
    mid0, mid1, mid2, fw0, fw1, fw2, mn0, mn1, mn2,
    last0, last1, last2, lf0, lf1, lf2, ln0, ln1, ln2,
    final, send, recv, load, pair_send, pair_recv,
):
    coords, core = position()
    own = (own0, own1, own2)
    far = ((far0, fw0, lf0), (far1, fw1, lf1), (far2, fw2, lf2))
    near = ((near0, mn0, ln0), (near1, mn1, ln1), (near2, mn2, ln2))
    sums = ((None, mid0, last0), (None, mid1, last1), (None, mid2, last2))
    width = QUARTER // 2

    def axis_of(part, phase):
        return ORDERS[part][2 - phase]

    def source(part, phase, shift, half):
        axis = axis_of(part, phase)
        at = lax.rem(coords[axis] + shift, RING)
        columns = pl.ds(half * width, width)
        if phase == 0:
            first, count = PARTS[part]
            index = [slice(None)] * 3
            index[axis] = at
            return t_ref.at[index[0], index[1], index[2], pl.ds(first, count), columns]
        if phase == 1:
            rest = [a for a in range(3) if a != axis_of(part, 0)]
            if rest[0] == axis:
                return sums[part][1].at[at, :, :, columns]
            return sums[part][1].at[:, at, :, columns]
        return sums[part][2].at[at, :, columns]

    loads = []
    for part in range(3):
        for slot, (shift, half) in enumerate(((0, 0), (0, 1), (1, 0), (3, 1))):
            c = pltpu.make_async_copy(
                source(part, 0, shift, half), own[part].at[slot], load.at[part, slot]
            )
            c.start()
            loads.append(c)
    meet(coords, core)
    sent = []

    def push(part, phase, which, src, dst, by):
        c = pltpu.make_async_remote_copy(
            src,
            dst,
            send.at[part, phase, which],
            recv.at[part, phase, which],
            device(moved(coords, axis_of(part, phase), by), core),
            MESH,
        )
        c.start()
        sent.append(c)

    def arrived(part, phase, which, ref):
        pltpu.make_async_copy(ref, ref, recv.at[part, phase, which]).wait()

    def begin(part, phase):
        f, n = far[part][phase], near[part][phase]
        push(part, phase, 0, source(part, phase, 2, 0), f.at[0], 1)
        push(part, phase, 1, source(part, phase, 2, 1), f.at[1], 3)
        push(part, phase, 2, source(part, phase, 1, 1), n.at[1], 1)
        push(part, phase, 3, source(part, phase, 3, 0), n.at[2], 3)

    def held(part, phase, slot):
        if phase == 0:
            return own[part].at[slot]
        shift, half = ((0, 0), (0, 1), (1, 0), (3, 1))[slot]
        return source(part, phase, shift, half)

    def each(phase, fn):
        if phase == 0:

            def body(i, carry):
                fn((lax.div(i, 4), lax.rem(i, 4)))
                return carry

            lax.fori_loop(0, 16, body, 0)
        elif phase == 1:

            def body(i, carry):
                fn((i,))
                return carry

            lax.fori_loop(0, 4, body, 0)
        else:
            fn(())

    def forward(part, phase):
        f, n = far[part][phase], near[part][phase]
        for slot, (which, held_slot, dst, by) in enumerate(((0, 2, 0, 1), (1, 3, 3, 3))):
            arrived(part, phase, which, f.at[slot])
            mine = held(part, phase, held_slot)
            if phase == 0:
                loads[4 * part + held_slot].wait()

            def add(index, slot=slot, mine=mine):
                a = f[(slot, *index)].astype(jnp.float32) + mine[index].astype(jnp.float32)
                f[(slot, *index)] = a.astype(f.dtype)

            each(phase, add)
            push(part, phase, 4 + slot, f.at[slot], n.at[dst], by)

    def finish(part, phase):
        n = near[part][phase]
        arrived(part, phase, 2, n.at[1])
        arrived(part, phase, 3, n.at[2])
        arrived(part, phase, 4, n.at[0])
        arrived(part, phase, 5, n.at[3])
        for half in range(2):
            if phase == 0:
                loads[4 * part + half].wait()
            mine = held(part, phase, half)

            def add(index, half=half, mine=mine):
                a = mine[index].astype(jnp.float32) + n[(half, *index)].astype(jnp.float32)
                a = a + n[(2 + half, *index)].astype(jnp.float32)
                columns = slice(half * width, (half + 1) * width)
                if phase == 2:
                    first, count = PARTS[part]
                    final[half, first : first + count, :] = a
                else:
                    dst = sums[part][phase + 1]
                    dst[(*index, slice(None), columns)] = a.astype(dst.dtype)

            each(phase, add)

    for part in range(3):
        begin(part, 0)
    for phase in range(3):
        for part in range(3):
            forward(part, phase)
        for part in range(3):
            finish(part, phase)
            if phase < 2:
                begin(part, phase + 1)
    swap = pltpu.make_async_remote_copy(
        final.at[1 - core],
        out_ref.at[pl.ds(pl.multiple_of(core * HALF, HALF), HALF)],
        pair_send,
        pair_recv,
        device(coords, 1 - core),
        MESH,
    )
    swap.start()
    out_ref[pl.ds(pl.multiple_of(core * HALF, HALF), HALF), :] = final[core]
    for c in sent:
        c.wait_send()
    swap.wait()


def reduce_terms(partial):
    width = QUARTER // 2
    rows = [count for _, count in PARTS]

    def buffers(lead, dims, dtype):
        return [pltpu.VMEM((*lead, *dims, r, width), dtype) for r in rows]

    def whole(dims, dtype):
        return [pltpu.VMEM((*dims, r, QUARTER), dtype) for r in rows]

    b16, f32 = jnp.bfloat16, jnp.float32
    return pl.pallas_call(
        reduce_kernel,
        out_shape=jax.ShapeDtypeStruct((L, COLS), jnp.float32),
        in_specs=[pl.BlockSpec(memory_space=pl.ANY)],
        out_specs=pl.BlockSpec(memory_space=pltpu.VMEM),
        scratch_shapes=[
            *buffers((4,), (4, 4), b16),
            *buffers((2,), (4, 4), b16),
            *buffers((4,), (4, 4), b16),
            *whole((4, 4), b16),
            *buffers((2,), (4,), b16),
            *buffers((4,), (4,), b16),
            *whole((4,), f32),
            *buffers((2,), (), f32),
            *buffers((4,), (), f32),
            pltpu.VMEM((2, HALF, width), f32),
            pltpu.SemaphoreType.DMA((3, 3, 6)),
            pltpu.SemaphoreType.DMA((3, 3, 6)),
            pltpu.SemaphoreType.DMA((3, 4)),
            pltpu.SemaphoreType.DMA,
            pltpu.SemaphoreType.DMA,
        ],
        compiler_params=pltpu.CompilerParams(
            collective_id=1, has_side_effects=True, vmem_limit_bytes=60 * 1024 * 1024
        ),
    )(partial)


def shards(grads, block_expert, sketch):
    own = sketch[0]
    owners = block_expert[:, 0]
    theirs = lax.ppermute(owners, "dp", [(k, k ^ 1) for k in range(N_DP)])
    basis, other = gather(own, grads)
    count, slots = slot_table(jnp.concatenate([owners, theirs]))
    partial = local_terms(count, slots, basis, grads, other)
    term = reduce_terms(partial)
    basis_gram = lax.psum(mm_nt(own, own), "dp")
    average = float(BLOCK * NBLK * N_DP)
    unscaled = jnp.dot(basis_gram, own.astype(jnp.float32), precision=HIGHEST) + term / average
    gram = lax.psum(
        lax.dot_general(unscaled, unscaled, (((1,), (1,)), ((), ())), precision=HIGHEST), "dp"
    )
    eye = jnp.eye(L, dtype=jnp.float32)
    total = jnp.trace(gram) + EPSILON
    a = gram / total
    q = None
    for step in range(ITERS):
        p = 1.5 * eye - 0.5 * a
        q = p if q is None else jnp.dot(p, q, precision=HIGHEST)
        if step < ITERS - 1:
            a = jnp.dot(jnp.dot(p, a, precision=HIGHEST), p, precision=HIGHEST)
    factor = jnp.dot(q, unscaled * lax.rsqrt(total), precision=HIGHEST) * D**0.5
    return lax.all_gather(factor.astype(jnp.bfloat16), "dp", axis=1, tiled=True)[None]


def solution(mesh):
    in_specs = (P(("dp", "expert"), None), P(("dp", "expert"), None), P("expert", None, "dp"))
    out_specs = P("expert", None, None)
    return jax.shard_map(shards, mesh=mesh, in_specs=in_specs, out_specs=out_specs, check_vma=False)
```

time: 782 us -> 321 us (0.41)
  waiting for transfers between devices: 372 us -> 82.8 us
  Pallas kernels: 0 us -> 203 us
  blocking collectives: 195 us -> 0 us
  matrix products: 115 us -> 14 us
  local copies, waits for them, and re-layouts: 52.1 us -> 3.31 us
  other arithmetic: 24.4 us -> 2.23 us
    all_to_all x1 -> x0, waiting for transfers between devices: 295 us -> none  [cut_exchange(): lax.all_to_all(piece, axis, split_axis=0, concat_axis=0, tiled=True)]
    pallas_call x0 -> x3, Pallas kernels: none -> 203 us  [the longest x1 88 us: reduce_terms(): pl.pallas_call(reduce_kernel, out_shape=jax.ShapeDtypeStruct((L, COLS), j...]
    all_to_all x1 -> x0, blocking collectives: 195 us -> none  [cut_exchange(): lax.all_to_all(piece, axis, split_axis=0, concat_axis=0, tiled=True)]
    dot_general x13 -> x16, matrix products: 115 us -> 14 us  [the longest x8 5.22 us: shards(): a = jnp.dot(jnp.dot(p, a, precision=HIGHEST), p, precision=HIGHEST)]
    all_gather x1, waiting for transfers between devices: 0.02 us -> 27.1 us  [shards(): lax.all_gather(factor.astype(jnp.bfloat16), 'dp', axis=1, tiled=True)[None]]
    concatenate x1, other arithmetic: 22.8 us -> 0.08 us  [shards(): count, slots = slot_table(jnp.concatenate([owners, theirs]))]
    scatter x1 -> x0, local copies, waits for them, and re-layouts: 21.4 us -> none  [shards(): jnp.zeros((experts * CAP, BLOCK, columns), jnp.bfloat16).at[targets]]
    psum x1 -> x2, waiting for transfers between devices: 75.7 us -> 55.7 us  [the longest x1 55.6 us: shards(): lax.psum(lax.dot_general(unscaled, unscaled, (((1,), (1,)), ((), ())), pr...]
  transfers between devices with their start and end apart: 3 -> 4, of which waited for: 2 -> 2; matrix products, arithmetic and copies ran while one was open for 3% -> 1% of each run, Pallas kernels for 0% -> 63%
where the time goes in v1:
time: 321 us; the launch traced here: 320 us
  Pallas kernels  203 us (63%)
  waiting for transfers between devices  82.8 us (26%)
  matrix products  14 us (4%)
  between operations  14 us (4%)
  local copies, waits for them, and re-layouts  3.31 us (1%)
    pallas_call x1, Pallas kernels, reduce_terms(): pl.pallas_call(reduce_kernel, out_shape=jax.ShapeDtypeStruct((L, COLS), j...  88 us
    pallas_call x1, Pallas kernels, gather(): pl.pallas_call(gather_kernel, out_shape=(jax.ShapeDtypeStruct((4, 4, 4, H...  82.2 us
    psum x1, waiting for transfers between devices, shards(): lax.psum(lax.dot_general(unscaled, unscaled, (((1,), (1,)), ((), ())), pr...  55.6 us
    pallas_call x1, Pallas kernels, local_terms(): pl.pallas_call(term_kernel, grid_spec=grid_spec, out_shape=jax.ShapeDtype...  32.5 us
    all_gather x1, waiting for transfers between devices, shards(): lax.all_gather(factor.astype(jnp.bfloat16), 'dp', axis=1, tiled=True)[None]  27.1 us
  transfers between devices with their start and end apart: 4, of which 2 were waited for; matrix products, arithmetic and copies ran while one was open for 1% of the time, Pallas kernels for 63%

profile of v1, /device:TPU:1, one launch (start us, length us, event | category | flops | bytes accessed | tf_op | source)
XLA Modules:
  0.0 320.5 jit_solution(12512416141485354151)
XLA Ops:
  6.5 0.0 copy-start.1
  6.5 0.0 all-reduce.3.cloned.1.call-start
  6.5 1.4 collective-permute-start
  7.9 2.0 fusion.52
  9.9 0.0 all-reduce.3.cloned.1.call-update
  9.9 0.0 all-reduce.5.cloned.1.call-start
  10.0 82.2 %shard_map.37 = (bf16[4,4,4,128,1024]{4,3,2,1,0:T(8,128)(2,1)}, bf16[1024,4096]{1,0:T(8,128)(2,1)}) custom-call(bf16[256,512]{1,0:T(8,128)(2,1)} %bitcast.26, bf16[1024,4096]{1,0:T(8,128)(2,1)} %own_ref.1), custom_call_target="tpu_custom_call" | custom-call | tf_op jit(solution)/shard_map/pallas_call | solution.py:130
  92.2 0.0 collective-permute-done
  92.3 0.0 copy-done.1
  92.3 0.1 pad_add_fusion.1
  92.4 0.4 convert_reduce_fusion
  92.7 0.2 select_reduce_fusion.4
  92.9 0.1 copy.6
  93.0 0.1 reshape.31.slot_ref
  93.1 32.5 %shard_map.38.t_ref = bf16[4,4,4,128,1024]{4,3,2,1,0:T(8,128)(2,1)} custom-call(s32[16]{0:T(128)S(1)} %get-tuple-element.13.count_ref, s32[64]{0:T(128)S(1)} %reshape.31.slot_ref, bf16[1024,4096]{1,0:T(8,128)(2,1)} %own_ref.1, bf16[1024,4096]{1,0:T(8,128)(2,1)} %get-tuple-element.7.other_ref, bf16[4,4,4,128,1024]{4,3,2,1,0:T(8,128)(2,1)} %get-tuple-element.8.s_ref), custom_call_target="tpu_custom_call" | custom-call | flops 4294967296 | bytes 50331648 | tf_op jit(solution)/shard_map/pallas_call | solution.py:226
  125.6 0.0 copy-start
  125.6 88.0 %shard_map.39 = f32[256,512]{1,0:T(8,128)} custom-call(bf16[4,4,4,128,1024]{4,3,2,1,0:T(8,128)(2,1)} %shard_map.38.t_ref), custom_call_target="tpu_custom_call" | custom-call | tf_op jit(solution)/shard_map/pallas_call | solution.py:402
  213.6 0.0 all-reduce.3.cloned.1.call-done
  213.6 0.0 copy-done
  213.6 1.5 convolution_add_fusion
  215.2 1.3 fusion.87
  216.5 0.0 all-reduce.5.cloned.1.call-update
  216.5 0.0 all-gather.2.cloned.1.call-start
  216.6 55.6 %all-reduce.5.cloned.1.call-done = f32[256,256]{1,0:T(8,128)} async-done(((f32[256,256]{1,0:T(8,128)}), f32[256,256]{1,0:T(8,128)}) %all-reduce.5.cloned.1.call-update) | async-done | bytes 262160 | tf_op jit(solution)/shard_map/psum | solution.py:441
  272.2 1.6 select_reduce_fusion
  274.5 1.4 fusion.8
  275.9 1.4 fusion.7
  277.3 0.4 fusion.10
  277.7 0.4 fusion.9
  278.1 0.4 fusion.13
  278.5 1.4 fusion.6
  279.9 0.4 fusion.11
  280.3 0.4 fusion.12
  280.8 0.4 fusion.5
  281.2 0.4 fusion.4
  281.6 0.4 fusion.1
  282.0 0.4 fusion.88
  282.4 1.3 fusion
  283.7 0.0 all-gather.2.cloned.1.call-update
  283.7 27.1 %all-gather.2.cloned.1.call-done = bf16[256,4096]{1,0:T(8,128)(2,1)} async-done(((bf16[256,512]{1,0:T(8,128)(2,1)}), bf16[256,4096]{1,0:T(8,128)(2,1)}) %all-gather.2.cloned.1.call-update) | async-done | bytes 2097168 | tf_op jit(solution)/shard_map/all_gather | solution.py:454
  310.8 3.1 copy.10
  (3 shorter events, 0.0 us)
Async XLA Ops:
  6.5 85.7 %copy-start.1 = (s32[8,1]{0,1:T(1,128)S(1)}, s32[8,1]{0,1:T(1,128)}, u32[]{:S(2)}) copy-start(s32[8,1]{0,1:T(1,128)} %param.4) | copy-start | bytes 100
  6.5 207.1 %all-reduce.3.cloned.1.call-start = ((), (), s32[]{:S(2)}) async-start(), calls=%async_computation | async-start | bytes 524288 | tf_op jit(solution)/shard_map/psum | solution.py:438
  6.5 85.7 %collective-permute-start = (s32[8]{0:T(128)}, s32[8]{0:T(128)S(1)}, u32[]{:S(2)}, u32[]{:S(2)}) collective-permute-start(s32[8]{0:T(128)} %bitcast.32), channel_id=1, source_target_pairs={{0,16},{16,0},{32,48},{48,32},{64,80},{80,64},{96,112},{112,96},{1... | collective-permute-start | bytes 104 | tf_op jit(solution)/shard_map/ppermute | solution.py:433
  9.9 262.3 %all-reduce.5.cloned.1.call-start = ((), (), s32[]{:S(2)}) async-start(), calls=%async_computation.1 | async-start | bytes 524288 | tf_op jit(solution)/shard_map/psum | solution.py:441
  125.6 88.1 %copy-start = (bf16[1,256,512]{2,1,0:T(8,128)(2,1)S(1)}, bf16[1,256,512]{2,1,0:T(8,128)(2,1)}, u32[]{:S(2)}) copy-start(bf16[1,256,512]{2,1,0:T(8,128)(2,1)} %param.5) | copy-start | bytes 786436
  216.5 94.3 %all-gather.2.cloned.1.call-start = ((), (), s32[]{:S(2)}) async-start(), calls=%async_computation.2 | async-start | bytes 2359296 | tf_op jit(solution)/shard_map/all_gather | solution.py:454
Sparse Core Ops, SparseCore 0:
  10.1 62.4 all-reduce.2
  216.6 55.5 all-reduce.4
  283.9 26.8 all-gather.1

commit v2 on v1

--- a/solution.py
+++ b/solution.py
@@ -42,9 +42,11 @@
     return tuple(lax.rem(c + by, RING) if k == axis else c for k, c in enumerate(coords))
 
 
-def meet(coords, core):
+def meet(coords, core, opposite=False):
     barrier = pltpu.get_barrier_semaphore()
     peers = [device(moved(coords, a, by), core) for a in range(3) for by in (1, 3)]
+    if opposite:
+        peers.append(device(moved(coords, 0, 2), core))
     peers.append(device(coords, 1 - core))
     for peer in peers:
         pl.semaphore_signal(barrier, inc=1, device_id=peer, device_id_type=MESH)
@@ -237,10 +239,10 @@
 
 
 def reduce_kernel(
-    t_ref, out_ref, own0, own1, own2, far0, far1, far2, near0, near1, near2,
+    t_ref, gram_ref, sketch_ref, out_ref, own0, own1, own2, far0, far1, far2, near0, near1, near2,
     mid0, mid1, mid2, fw0, fw1, fw2, mn0, mn1, mn2,
     last0, last1, last2, lf0, lf1, lf2, ln0, ln1, ln2,
-    final, send, recv, load, pair_send, pair_recv,
+    final, term, gp, gin, gx, gfull, send, recv, load, pair_send, pair_recv, x_send, x_recv,
 ):
     coords, core = position()
     own = (own0, own1, own2)
@@ -276,7 +278,7 @@
             )
             c.start()
             loads.append(c)
-    meet(coords, core)
+    meet(coords, core, opposite=True)
     sent = []
 
     def push(part, phase, which, src, dst, by):
@@ -373,22 +375,114 @@
             finish(part, phase)
             if phase < 2:
                 begin(part, phase + 1)
-    swap = pltpu.make_async_remote_copy(
-        final.at[1 - core],
-        out_ref.at[pl.ds(pl.multiple_of(core * HALF, HALF), HALF)],
-        pair_send,
-        pair_recv,
-        device(coords, 1 - core),
-        MESH,
-    )
-    swap.start()
-    out_ref[pl.ds(pl.multiple_of(core * HALF, HALF), HALF), :] = final[core]
+    partner = device(coords, 1 - core)
+    mine = pl.ds(pl.multiple_of(core * HALF, HALF), HALF)
+    theirs = pl.ds(pl.multiple_of((1 - core) * HALF, HALF), HALF)
+
+    def give(src, dst, which):
+        c = pltpu.make_async_remote_copy(
+            src, dst, pair_send.at[which], pair_recv.at[which], partner, MESH
+        )
+        c.start()
+        return c
+
+    def across(src, dst, which, by):
+        c = pltpu.make_async_remote_copy(
+            src, dst, x_send.at[which], x_recv.at[which], device(moved(coords, 0, by), core), MESH
+        )
+        c.start()
+        return c
+
+    swap = give(final.at[1 - core], term.at[mine], 0)
+    term[mine, :] = final[core]
+    product = two_pass(gram_ref[...], sketch_ref[...])
+    swap.wait()
+    average = float(BLOCK * NBLK * N_DP)
+    unscaled = product + term[...] / average
+    term[...] = unscaled
+    gp[...] = three_pass_nt(unscaled, unscaled)
+    swap = give(gp.at[theirs], gin, 1)
+    swap.wait()
+    gin[...] = gin[...] + gp[mine, :]
+    sends = [across(gin, gx.at[by - 1], by - 1, by) for by in (1, 2, 3)]
+    for c in sends:
+        c.wait()
+    gfull[mine, :] = (gin[...] + gx[1]) + (gx[0] + gx[2])
+    swap = give(gfull.at[mine], gfull.at[mine], 2)
+    swap.wait()
+    gram = gfull[...]
+    row = lax.broadcasted_iota(jnp.int32, (L, L), 0)
+    col = lax.broadcasted_iota(jnp.int32, (L, L), 1)
+    diagonal = row == col
+    total = jnp.sum(jnp.where(diagonal, gram, 0.0)) + EPSILON
+    total = jnp.full((1, 1), total, jnp.float32)
+    a = gram / total
+    q = None
+    for step in range(ITERS):
+        p = jnp.where(diagonal, 1.5, 0.0) - 0.5 * a
+        q = p if q is None else three_pass(p, q)
+        if step < ITERS - 1:
+            a = three_pass(three_pass(p, a), p)
+    scale = D**0.5 * lax.rsqrt(total)
+    factor = three_pass(q, term[...] * scale)
+
+    def chunk(shift, core_of):
+        index = 2 * lax.rem(coords[0] + shift, RING) + core_of
+        return pl.ds(pl.multiple_of(index * COLS, COLS), COLS)
+
+    def piece(shift, rows=slice(None)):
+        return out_ref.at[rows, chunk(shift, core)]
+
+    out_ref[:, chunk(0, core)] = factor.astype(jnp.bfloat16)
+    upper, lower = pl.ds(0, HALF), pl.ds(HALF, HALF)
+    right = across(piece(0), piece(0), 3, 1)
+    left = across(piece(0), piece(0), 4, 3)
+    gives = [give(piece(0), piece(0), 3)]
+    right.wait_recv()
+    on_right = across(piece(3, upper), piece(3, upper), 5, 1)
+    gives.append(give(piece(3), piece(3), 4))
+    left.wait_recv()
+    on_left = across(piece(1, lower), piece(1, lower), 6, 3)
+    gives.append(give(piece(1), piece(1), 5))
+    on_right.wait_recv()
+    gives.append(give(piece(2, upper), piece(2, upper), 6))
+    on_left.wait_recv()
+    gives.append(give(piece(2, lower), piece(2, lower), 7))
+    for c in (right, left, on_right, on_left):
+        c.wait_send()
+    for c in gives:
+        c.wait()
     for c in sent:
         c.wait_send()
-    swap.wait()
-
-
-def reduce_terms(partial):
+
+
+def split(a):
+    high = a.astype(jnp.bfloat16)
+    return high, (a - high.astype(jnp.float32)).astype(jnp.bfloat16)
+
+
+def mm(a, b):
+    return jnp.dot(a, b, preferred_element_type=jnp.float32)
+
+
+def two_pass(a, b):
+    high, low = split(a)
+    return mm(high, b) + mm(low, b)
+
+
+def three_pass(a, b):
+    ah, al = split(a)
+    bh, bl = split(b)
+    return mm(ah, bh) + (mm(ah, bl) + mm(al, bh))
+
+
+def three_pass_nt(a, b):
+    ah, al = split(a)
+    bh, bl = split(b)
+    return mm_nt(ah, bh) + (mm_nt(ah, bl) + mm_nt(al, bh))
+
+
+def reduce_terms(partial, basis_gram, own):
     width = QUARTER // 2
     rows = [count for _, count in PARTS]
 
@@ -401,8 +495,12 @@
     b16, f32 = jnp.bfloat16, jnp.float32
     return pl.pallas_call(
         reduce_kernel,
-        out_shape=jax.ShapeDtypeStruct((L, COLS), jnp.float32),
-        in_specs=[pl.BlockSpec(memory_space=pl.ANY)],
+        out_shape=jax.ShapeDtypeStruct((L, D), jnp.bfloat16),
+        in_specs=[
+            pl.BlockSpec(memory_space=pl.ANY),
+            pl.BlockSpec(memory_space=pltpu.VMEM),
+            pl.BlockSpec(memory_space=pltpu.VMEM),
+        ],
         out_specs=pl.BlockSpec(memory_space=pltpu.VMEM),
         scratch_shapes=[
             *buffers((4,), (4, 4), b16),
@@ -415,43 +513,34 @@
             *buffers((2,), (), f32),
             *buffers((4,), (), f32),
             pltpu.VMEM((2, HALF, width), f32),
+            pltpu.VMEM((L, COLS), f32),
+            pltpu.VMEM((L, L), f32),
+            pltpu.VMEM((HALF, L), f32),
+            pltpu.VMEM((3, HALF, L), f32),
+            pltpu.VMEM((L, L), f32),
             pltpu.SemaphoreType.DMA((3, 3, 6)),
             pltpu.SemaphoreType.DMA((3, 3, 6)),
             pltpu.SemaphoreType.DMA((3, 4)),
-            pltpu.SemaphoreType.DMA,
-            pltpu.SemaphoreType.DMA,
+            pltpu.SemaphoreType.DMA((8,)),
+            pltpu.SemaphoreType.DMA((8,)),
+            pltpu.SemaphoreType.DMA((7,)),
+            pltpu.SemaphoreType.DMA((7,)),
         ],
         compiler_params=pltpu.CompilerParams(
             collective_id=1, has_side_effects=True, vmem_limit_bytes=60 * 1024 * 1024
         ),
-    )(partial)
+    )(partial, basis_gram, own)
 
 
 def shards(grads, block_expert, sketch):
     own = sketch[0]
     owners = block_expert[:, 0]
     theirs = lax.ppermute(owners, "dp", [(k, k ^ 1) for k in range(N_DP)])
+    basis_gram = lax.psum(mm_nt(own, own), "dp")
     basis, other = gather(own, grads)
     count, slots = slot_table(jnp.concatenate([owners, theirs]))
     partial = local_terms(count, slots, basis, grads, other)
-    term = reduce_terms(partial)
-    basis_gram = lax.psum(mm_nt(own, own), "dp")
-    average = float(BLOCK * NBLK * N_DP)
-    unscaled = jnp.dot(basis_gram, own.astype(jnp.float32), precision=HIGHEST) + term / average
-    gram = lax.psum(
-        lax.dot_general(unscaled, unscaled, (((1,), (1,)), ((), ())), precision=HIGHEST), "dp"
-    )
-    eye = jnp.eye(L, dtype=jnp.float32)
-    total = jnp.trace(gram) + EPSILON
-    a = gram / total
-    q = None
-    for step in range(ITERS):
-        p = 1.5 * eye - 0.5 * a
-        q = p if q is None else jnp.dot(p, q, precision=HIGHEST)
-        if step < ITERS - 1:
-            a = jnp.dot(jnp.dot(p, a, precision=HIGHEST), p, precision=HIGHEST)
-    factor = jnp.dot(q, unscaled * lax.rsqrt(total), precision=HIGHEST) * D**0.5
-    return lax.all_gather(factor.astype(jnp.bfloat16), "dp", axis=1, tiled=True)[None]
+    return reduce_terms(partial, basis_gram, own)[None]
 
 
 def solution(mesh):

time: 321 us -> 254 us (0.79)
  waiting for transfers between devices: 82.8 us -> 0.04 us
  Pallas kernels: 203 us -> 232 us
  matrix products: 14 us -> 1.99 us
    psum x1 -> x0, waiting for transfers between devices: 55.6 us -> none  [shards(): lax.psum(lax.dot_general(unscaled, unscaled, (((1,), (1,)), ((), ())), pr...]
    pallas_call x1, Pallas kernels: 88 us -> 119 us  [reduce_terms(): pl.pallas_call(reduce_kernel, out_shape=jax.ShapeDtypeStruct((L, D), jnp....]
    all_gather x1 -> x0, waiting for transfers between devices: 27.1 us -> none  [shards(): lax.all_gather(factor.astype(jnp.bfloat16), 'dp', axis=1, tiled=True)[None]]
    dot_general x15 -> x0, matrix products: 12 us -> none  [the longest x8 5.22 us: shards(): a = jnp.dot(jnp.dot(p, a, precision=HIGHEST), p, precision=HIGHEST)]
  transfers between devices with their start and end apart: 4 -> 2, of which waited for: 2 -> 0; matrix products, arithmetic and copies ran while one was open for 1% -> 1% of each run, Pallas kernels for 63% -> 45%
where the time goes in v2:
time: 254 us; the launch traced here: 253 us
  Pallas kernels  232 us (91%)
  between operations  13.5 us (5%)
  local copies, waits for them, and re-layouts  3.31 us (1%)
    pallas_call x1, Pallas kernels, reduce_terms(): pl.pallas_call(reduce_kernel, out_shape=jax.ShapeDtypeStruct((L, D), jnp....  119 us
    pallas_call x1, Pallas kernels, gather(): pl.pallas_call(gather_kernel, out_shape=(jax.ShapeDtypeStruct((4, 4, 4, H...  82.2 us
    pallas_call x1, Pallas kernels, local_terms(): pl.pallas_call(term_kernel, grid_spec=grid_spec, out_shape=jax.ShapeDtype...  31.1 us
  transfers between devices with their start and end apart: 2, of which 0 were waited for; matrix products, arithmetic and copies ran while one was open for 1% of the time, Pallas kernels for 45%

profile of v2, /device:TPU:1, one launch (start us, length us, event | category | flops | bytes accessed | tf_op | source)
XLA Modules:
  0.0 253.3 jit_solution(12669018299533060969)
XLA Ops:
  6.5 0.0 copy-start
  6.5 0.0 all-reduce.2.cloned.1.call-start
  6.5 1.4 collective-permute-start
  7.9 2.0 fusion.4
  9.9 0.0 all-reduce.2.cloned.1.call-update
  10.0 82.2 %shard_map.37 = (bf16[4,4,4,128,1024]{4,3,2,1,0:T(8,128)(2,1)}, bf16[1024,4096]{1,0:T(8,128)(2,1)}) custom-call(bf16[256,512]{1,0:T(8,128)(2,1)} %bitcast.10, bf16[1024,4096]{1,0:T(8,128)(2,1)} %own_ref.1), custom_call_target="tpu_custom_call" | custom-call | tf_op jit(solution)/shard_map/pallas_call | solution.py:132
  92.2 0.0 collective-permute-done
  92.2 0.0 copy-done
  92.2 0.1 pad_add_fusion.1
  92.3 0.4 convert_reduce_fusion
  92.7 0.2 select_reduce_fusion.3
  92.9 0.1 copy.6
  93.0 0.1 reshape.31.slot_ref
  93.0 31.1 %shard_map.38.t_ref = bf16[4,4,4,128,1024]{4,3,2,1,0:T(8,128)(2,1)} custom-call(s32[16]{0:T(128)S(1)} %get-tuple-element.13.count_ref, s32[64]{0:T(128)S(1)} %reshape.31.slot_ref, bf16[1024,4096]{1,0:T(8,128)(2,1)} %own_ref.1, bf16[1024,4096]{1,0:T(8,128)(2,1)} %get-tuple-element.7.other_ref, bf16[4,4,4,128,1024]{4,3,2,1,0:T(8,128)(2,1)} %get-tuple-element.8.s_ref), custom_call_target="tpu_custom_call" | custom-call | flops 4294967296 | bytes 50331648 | tf_op jit(solution)/shard_map/pallas_call | solution.py:228
  124.2 0.0 all-reduce.2.cloned.1.call-done.gram_ref
  124.2 119.1 %shard_map.39 = bf16[256,4096]{1,0:T(8,128)(2,1)} custom-call(bf16[4,4,4,128,1024]{4,3,2,1,0:T(8,128)(2,1)} %shard_map.38.t_ref, f32[256,256]{1,0:T(8,128)} %all-reduce.2.cloned.1.call-done.gram_ref, bf16[256,512]{1,0:T(8,128)(2,1)} %bitcast.11), custom_call_target="tpu_custom_call" | custom-call | tf_op jit(solution)/shard_map/pallas_call | solution.py:496
  243.3 3.1 %copy.9 = bf16[1,256,4096]{2,1,0:T(8,128)(2,1)} copy(bf16[1,256,4096]{2,1,0:T(8,128)(2,1)} %bitcast.9) | data formatting | bytes 4194304
  (3 shorter events, 0.0 us)
Async XLA Ops:
  6.5 85.7 %copy-start = (s32[8,1]{0,1:T(1,128)S(1)}, s32[8,1]{0,1:T(1,128)}, u32[]{:S(2)}) copy-start(s32[8,1]{0,1:T(1,128)} %param.4) | copy-start | bytes 100
  6.5 117.7 %all-reduce.2.cloned.1.call-start = ((), (), s32[]{:S(2)}) async-start(), calls=%async_computation | async-start | bytes 524288 | tf_op jit(solution)/shard_map/psum | solution.py:539
  6.5 85.7 %collective-permute-start = (s32[8]{0:T(128)}, s32[8]{0:T(128)S(1)}, u32[]{:S(2)}, u32[]{:S(2)}) collective-permute-start(s32[8]{0:T(128)} %bitcast.16), channel_id=1, source_target_pairs={{0,16},{16,0},{32,48},{48,32},{64,80},{80,64},{96,112},{112,96},{1... | collective-permute-start | bytes 104 | tf_op jit(solution)/shard_map/ppermute | solution.py:538
Sparse Core Ops, SparseCore 0:
  10.1 62.3 all-reduce.1

commit v3 on v2

--- a/solution.py
+++ b/solution.py
@@ -53,11 +53,62 @@
     pl.semaphore_wait(barrier, len(peers))
 
 
+PIECES = tuple((32 * k, 32, 0, QUARTER, ORDERS[k], True) for k in range(3)) + tuple(
+    (96, 32, first, count, ORDERS[k], False)
+    for k, (first, count) in enumerate(((0, 384), (384, 384), (768, 256)))
+)
+GATHER_COPIES = 4 * sum(6 if piece[5] else 3 for piece in PIECES)
+ALL = slice(None)
+
+
+class GatherRing:
+    def __init__(self, env, piece, fixed, axis):
+        self.env, self.piece, self.fixed, self.axis = env, piece, fixed, axis
+        self.ids = [env["count"] + k for k in range(4)]
+        env["count"] += 4
+
+    def view(self, shift, half=None):
+        coords = self.env["coords"]
+        row, rows, col, cols = self.piece[:4]
+        if half is not None:
+            row, rows = row + half * (rows // 2), rows // 2
+        index = []
+        for axis in range(3):
+            step = shift if axis == self.axis else self.fixed.get(axis, 0)
+            index.append(ALL if step is ALL else pl.ds(lax.rem(coords[axis] + step, RING), 1))
+        return self.env["ref"].at[(*index, pl.ds(row, rows), pl.ds(col, cols))]
+
+    def push(self, which, ref, by):
+        env, k = self.env, self.ids[which]
+        target = device(moved(env["coords"], self.axis, by), env["core"])
+        copy = pltpu.make_async_remote_copy(
+            ref, ref, env["send"].at[k], env["recv"].at[k], target, MESH
+        )
+        copy.start()
+        env["sent"].append(copy)
+
+    def arrived(self, which, ref):
+        pltpu.make_async_copy(ref, ref, self.env["recv"].at[self.ids[which]]).wait()
+
+    def start(self):
+        self.push(0, self.view(0), 1)
+        self.push(1, self.view(0), 3)
+
+    def forward(self):
+        self.arrived(0, self.view(3))
+        self.push(2, self.view(3, 0), 1)
+        self.arrived(1, self.view(1))
+        self.push(3, self.view(1, 1), 3)
+
+    def finish(self):
+        self.arrived(2, self.view(2, 0))
+        self.arrived(3, self.view(2, 1))
+
+
 def gather_kernel(sketch_ref, grads_ref, basis_ref, other_ref, send, recv, pair_send, pair_recv, local):
     coords, core = position()
     meet(coords, core)
     partner = device(coords, 1 - core)
-    mine = tuple(pl.ds(c, 1) for c in coords)
     cols = pl.ds(pl.multiple_of(core * COLS, COLS), COLS)
     own_rows = pl.ds(pl.multiple_of(core * HALF, HALF), HALF)
     other_rows = pl.ds(pl.multiple_of((1 - core) * HALF, HALF), HALF)
@@ -71,60 +122,49 @@
     swap = pltpu.make_async_remote_copy(
         grads_ref, other_ref, pair_send.at[1], pair_recv.at[1], partner, MESH
     )
-    swap.start()
     keep.wait()
     give.wait()
 
-    def view(part, phase, shift, half):
-        first, count = PARTS[part]
-        order = ORDERS[part]
-        index = list(mine)
-        for axis in order[:phase]:
-            index[axis] = slice(None)
-        axis = order[phase]
-        index[axis] = pl.ds(lax.rem(coords[axis] + shift, RING), 1)
-        columns = slice(None) if half is None else pl.ds(half * (QUARTER // 2), QUARTER // 2)
-        return basis_ref.at[index[0], index[1], index[2], pl.ds(first, count), columns]
-
-    def copy(part, phase, which, shift, half, by):
-        ref = view(part, phase, shift, half)
-        return pltpu.make_async_remote_copy(
-            ref,
-            ref,
-            send.at[part, phase, which],
-            recv.at[part, phase, which],
-            device(moved(coords, ORDERS[part][phase], by), core),
-            MESH,
-        )
-
-    def arrived(part, phase, which, shift, half):
-        ref = view(part, phase, shift, half)
-        pltpu.make_async_copy(ref, ref, recv.at[part, phase, which]).wait()
-
-    sent = []
-
-    def start(*args):
-        c = copy(*args)
-        c.start()
-        sent.append(c)
-
-    for part in range(3):
-        start(part, 0, 0, 0, None, 1)
-        start(part, 0, 1, 0, None, 3)
-    for phase in range(3):
-        for part in range(3):
-            arrived(part, phase, 0, 3, None)
-            start(part, phase, 2, 3, 0, 1)
-            arrived(part, phase, 1, 1, None)
-            start(part, phase, 3, 1, 1, 3)
-        for part in range(3):
-            arrived(part, phase, 2, 2, 0)
-            arrived(part, phase, 3, 2, 1)
-            if phase < 2:
-                start(part, phase + 1, 0, 0, None, 1)
-                start(part, phase + 1, 1, 0, None, 3)
-    for c in sent:
-        c.wait_send()
+    env = dict(coords=coords, core=core, ref=basis_ref, send=send, recv=recv, sent=[], count=0)
+    first, second, third = [], [], []
+    for piece in PIECES:
+        a1, a2, a3 = piece[4]
+        first.append(GatherRing(env, piece, {}, a1))
+        second.append(GatherRing(env, piece, {a1: ALL}, a2))
+        steps = (0, 3, 1, 2) if piece[5] else (ALL,)
+        third.append([GatherRing(env, piece, {a1: ALL, a2: k}, a3) for k in steps])
+    sliced = [k for k, piece in enumerate(PIECES) if piece[5]]
+    for ring in first:
+        ring.start()
+    swap.start()
+    for ring in first:
+        ring.forward()
+    for k, ring in enumerate(first):
+        ring.finish()
+        second[k].start()
+    for k in sliced:
+        third[k][0].start()
+    for ring in second:
+        ring.forward()
+    for k in sliced:
+        third[k][1].start()
+        third[k][2].start()
+    for k in sliced:
+        third[k][0].forward()
+    for k, ring in enumerate(second):
+        ring.finish()
+        third[k][-1].start()
+    for step in (1, 2, 3):
+        for k in sliced:
+            third[k][step].forward()
+    for k in range(len(PIECES)):
+        if k not in sliced:
+            third[k][0].forward()
+    for rings in third:
+        for ring in rings:
+            ring.finish()
+    for copy in env["sent"]:
+        copy.wait_send()
     swap.wait()
 
 
@@ -141,8 +181,8 @@
         ],
         out_specs=(pl.BlockSpec(memory_space=pl.ANY), pl.BlockSpec(memory_space=pl.ANY)),
         scratch_shapes=[
-            pltpu.SemaphoreType.DMA((3, 3, 4)),
-            pltpu.SemaphoreType.DMA((3, 3, 4)),
+            pltpu.SemaphoreType.DMA((GATHER_COPIES,)),
+            pltpu.SemaphoreType.DMA((GATHER_COPIES,)),
             pltpu.SemaphoreType.DMA((2,)),
             pltpu.SemaphoreType.DMA((2,)),
             pltpu.SemaphoreType.DMA,
@@ -151,19 +191,33 @@
     )(sketch, grads)
 
 
-def term_kernel(count_ref, slot_ref, own_ref, other_ref, s_ref, t_ref, g_ref, p_ref, sem):
+def term_kernel(count_ref, slot_ref, order_ref, own_ref, other_ref, s_ref, t_ref, g_ref, p_ref, sem):
     e = pl.program_id(0)
     count = count_ref[e]
-    rows_of = NBLK * BLOCK
+
+    def block_copy(b, src):
+        rows = pl.ds(pl.multiple_of(lax.rem(b, NBLK) * BLOCK, BLOCK), BLOCK)
+        place = pl.ds(pl.multiple_of(b * BLOCK, BLOCK), BLOCK)
+        return pltpu.make_async_copy(src.at[rows], g_ref.at[place], sem.at[b])
 
     @pl.when(e == 0)
     def _():
-        first = pltpu.make_async_copy(own_ref, g_ref.at[0:rows_of], sem.at[0])
-        second = pltpu.make_async_copy(other_ref, g_ref.at[rows_of : 2 * rows_of], sem.at[1])
-        first.start()
-        second.start()
-        first.wait()
-        second.wait()
+        for k in range(2 * NBLK):
+            b = order_ref[k]
+
+            @pl.when(b < NBLK)
+            def _(b=b):
+                block_copy(b, own_ref).start()
+
+            @pl.when(b >= NBLK)
+            def _(b=b):
+                block_copy(b, other_ref).start()
+
+    for j in range(4):
+
+        @pl.when(count > j)
+        def _(j=j):
+            block_copy(slot_ref[4 * e + j], own_ref).wait()
 
     def rows(j):
         return pl.ds(pl.multiple_of(slot_ref[4 * e + j] * BLOCK, BLOCK), BLOCK)
@@ -179,11 +233,11 @@
 
         @pl.when(count > 2 * k)
         def _(k=k):
-            acc = jnp.zeros((HALF, 2 * BLOCK), jnp.float32)
+            acc = jnp.zeros((2 * BLOCK, HALF), jnp.float32)
             for x in range(4):
-                acc += mm_nt(s_ref[x, 0, 0], pair(k, x * QUARTER, (x + 1) * QUARTER))
-            place = lax.broadcasted_iota(jnp.int32, acc.shape, 1) // BLOCK + 2 * k
-            p_ref[k] = jnp.where(place < count, acc, 0.0).astype(jnp.bfloat16)
+                acc += mm_nt(pair(k, x * QUARTER, (x + 1) * QUARTER), s_ref[x, 0, 0])
+            place = lax.broadcasted_iota(jnp.int32, acc.shape, 0) // BLOCK + 2 * k
+            p_ref[k] = jnp.where(place < count, acc, 0.0).T.astype(jnp.bfloat16)
 
     def emit(pairs):
         for x in range(4):
@@ -206,23 +260,28 @@
     blocks = owners.shape[0]
     b = jnp.arange(blocks, dtype=jnp.int32)
     rank = jnp.sum(hit[:, None, :] & (b[None, :] < b[:, None])[None], axis=2).astype(jnp.int32)
+    slot0 = jnp.sum(jnp.where(hit & (rank == 0), b[None, :], 0), axis=1)
     slots = [
-        jnp.sum(jnp.where(hit & (rank == j), b[None, :], 0), axis=1) for j in range(4)
+        jnp.where(count > j, jnp.sum(jnp.where(hit & (rank == j), b[None, :], 0), axis=1), slot0)
+        for j in range(4)
     ]
-    return count, jnp.stack(slots, axis=1).reshape(-1)
-
-
-def local_terms(count, slots, basis, grads, other):
+    key = owners * blocks + b
+    turn = jnp.sum((key[None, :] < key[:, None]).astype(jnp.int32), axis=1)
+    order = jnp.sum(jnp.where(turn[None, :] == b[:, None], b[None, :], 0), axis=1)
+    return count, jnp.stack(slots, axis=1).reshape(-1), order
+
+
+def local_terms(count, slots, order, basis, grads, other):
     spec = pl.BlockSpec((4, 1, 1, HALF, QUARTER), lambda e, *_: (0, e // 4, e % 4, 0, 0))
     grid_spec = pltpu.PrefetchScalarGridSpec(
-        num_scalar_prefetch=2,
+        num_scalar_prefetch=3,
         grid=(EXPERTS,),
         in_specs=[pl.BlockSpec(memory_space=pl.ANY), pl.BlockSpec(memory_space=pl.ANY), spec],
         out_specs=spec,
         scratch_shapes=[
             pltpu.VMEM((2 * NBLK * BLOCK, D), jnp.bfloat16),
             pltpu.VMEM((2, HALF, 2 * BLOCK), jnp.bfloat16),
-            pltpu.SemaphoreType.DMA((2,)),
+            pltpu.SemaphoreType.DMA((2 * NBLK,)),
         ],
     )
     return pl.pallas_call(
@@ -235,14 +294,14 @@
         cost_estimate=pl.CostEstimate(
             flops=8 * NBLK * BLOCK * HALF * D, bytes_accessed=48 << 20, transcendentals=0
         ),
-    )(count, slots, grads, other, basis)
+    )(count, slots, order, grads, other, basis)
 
 
 def reduce_kernel(
-    t_ref, gram_ref, sketch_ref, out_ref, own0, own1, own2, far0, far1, far2, near0, near1, near2,
+    t_ref, basis_ref, sketch_ref, out_ref, own0, own1, own2, far0, far1, far2, near0, near1, near2,
     mid0, mid1, mid2, fw0, fw1, fw2, mn0, mn1, mn2,
     last0, last1, last2, lf0, lf1, lf2, ln0, ln1, ln2,
-    final, term, gp, gin, gx, gfull, send, recv, load, pair_send, pair_recv, x_send, x_recv,
+    final, whole, term, gp, gin, gx, gfull, send, recv, load, pair_send, pair_recv, x_send, x_recv,
 ):
     coords, core = position()
     own = (own0, own1, own2)
@@ -278,6 +337,10 @@
             )
             c.start()
             loads.append(c)
+    whole_own = pltpu.make_async_copy(
+        basis_ref.at[:, coords[1], coords[2]], whole.at[core], load.at[3, 0]
+    )
+    whole_own.start()
     meet(coords, core, opposite=True)
     sent = []
 
@@ -368,6 +431,22 @@
 
     for part in range(3):
         begin(part, 0)
+    whole_swap = pltpu.make_async_remote_copy(
+        basis_ref.at[:, coords[1], coords[2]],
+        whole.at[core],
+        pair_send.at[8],
+        pair_recv.at[8],
+        device(coords, 1 - core),
+        MESH,
+    )
+    whole_swap.start()
+    whole_own.wait()
+    whole_swap.wait()
+    gp[...] = jnp.zeros_like(gp)
+    for x in range(4):
+        for h in range(2):
+            gp[h * HALF : (h + 1) * HALF, 0:HALF] += mm_nt(whole[h, x], whole[0, x])
+            gp[h * HALF : (h + 1) * HALF, HALF:] += mm_nt(whole[h, x], whole[1, x])
     for phase in range(3):
         for part in range(3):
             forward(part, phase)
@@ -395,7 +474,7 @@
 
     swap = give(final.at[1 - core], term.at[mine], 0)
     term[mine, :] = final[core]
-    product = two_pass(gram_ref[...], sketch_ref[...])
+    product = two_pass(gp[...], sketch_ref[...])
     swap.wait()
     average = float(BLOCK * NBLK * N_DP)
     unscaled = product + term[...] / average
@@ -482,7 +561,7 @@
     return mm_nt(ah, bh) + (mm_nt(ah, bl) + mm_nt(al, bh))
 
 
-def reduce_terms(partial, basis_gram, own):
+def reduce_terms(partial, basis, own):
     width = QUARTER // 2
     rows = [count for _, count in PARTS]
 
@@ -498,7 +577,7 @@
         out_shape=jax.ShapeDtypeStruct((L, D), jnp.bfloat16),
         in_specs=[
             pl.BlockSpec(memory_space=pl.ANY),
-            pl.BlockSpec(memory_space=pltpu.VMEM),
+            pl.BlockSpec(memory_space=pl.ANY),
             pl.BlockSpec(memory_space=pltpu.VMEM),
         ],
         out_specs=pl.BlockSpec(memory_space=pltpu.VMEM),
@@ -513,6 +592,7 @@
             *buffers((2,), (), f32),
             *buffers((4,), (), f32),
             pltpu.VMEM((2, HALF, width), f32),
+            pltpu.VMEM((2, 4, HALF, QUARTER), b16),
             pltpu.VMEM((L, COLS), f32),
             pltpu.VMEM((L, L), f32),
             pltpu.VMEM((HALF, L), f32),
@@ -520,27 +600,26 @@
             pltpu.VMEM((L, L), f32),
             pltpu.SemaphoreType.DMA((3, 3, 6)),
             pltpu.SemaphoreType.DMA((3, 3, 6)),
-            pltpu.SemaphoreType.DMA((3, 4)),
-            pltpu.SemaphoreType.DMA((8,)),
-            pltpu.SemaphoreType.DMA((8,)),
+            pltpu.SemaphoreType.DMA((4, 4)),
+            pltpu.SemaphoreType.DMA((9,)),
+            pltpu.SemaphoreType.DMA((9,)),
             pltpu.SemaphoreType.DMA((7,)),
             pltpu.SemaphoreType.DMA((7,)),
         ],
         compiler_params=pltpu.CompilerParams(
             collective_id=1, has_side_effects=True, vmem_limit_bytes=60 * 1024 * 1024
         ),
-    )(partial, basis_gram, own)
+    )(partial, basis, own)
 
 
 def shards(grads, block_expert, sketch):
     own = sketch[0]
     owners = block_expert[:, 0]
     theirs = lax.ppermute(owners, "dp", [(k, k ^ 1) for k in range(N_DP)])
-    basis_gram = lax.psum(mm_nt(own, own), "dp")
     basis, other = gather(own, grads)
-    count, slots = slot_table(jnp.concatenate([owners, theirs]))
-    partial = local_terms(count, slots, basis, grads, other)
-    return reduce_terms(partial, basis_gram, own)[None]
+    count, slots, order = slot_table(jnp.concatenate([owners, theirs]))
+    partial = local_terms(count, slots, order, basis, grads, other)
+    return reduce_terms(partial, basis, own)[None]
 
 
 def solution(mesh):

time: 254 us -> 229 us (0.902)
  between operations: 13.5 us -> 0.07 us
  Pallas kernels: 232 us -> 223 us
    pallas_call x1, Pallas kernels: 82.2 us -> 75.8 us  [gather(): pl.pallas_call(gather_kernel, out_shape=(jax.ShapeDtypeStruct((4, 4, 4, H...]
    pallas_call x1, Pallas kernels: 119 us -> 116 us  [reduce_terms(): pl.pallas_call(reduce_kernel, out_shape=jax.ShapeDtypeStruct((L, D), jnp....]
  transfers between devices with their start and end apart: 2 -> 1, of which waited for: 0 -> 0; matrix products, arithmetic and copies ran while one was open for 1% -> 0% of each run, Pallas kernels for 45% -> 33%
where the time goes in v3:
time: 229 us; the launch traced here: 228 us
  Pallas kernels  223 us (97%)
  local copies, waits for them, and re-layouts  3.3 us (1%)
    pallas_call x1, Pallas kernels, reduce_terms(): pl.pallas_call(reduce_kernel, out_shape=jax.ShapeDtypeStruct((L, D), jnp....  116 us
    pallas_call x1, Pallas kernels, gather(): pl.pallas_call(gather_kernel, out_shape=(jax.ShapeDtypeStruct((4, 4, 4, H...  75.8 us
    pallas_call x1, Pallas kernels, local_terms(): pl.pallas_call(term_kernel, grid_spec=grid_spec, out_shape=jax.ShapeDtype...  31.1 us
  transfers between devices with their start and end apart: 1, of which 0 were waited for; matrix products, arithmetic and copies ran while one was open for 0% of the time, Pallas kernels for 33%

profile of v3, /device:TPU:1, one launch (start us, length us, event | category | flops | bytes accessed | tf_op | source)
XLA Modules:
  0.0 228.4 jit_solution(18098311991138633299)
XLA Ops:
  0.0 0.0 copy-start
  0.0 1.4 collective-permute-start
  1.4 75.8 %shard_map.37 = (bf16[4,4,4,128,1024]{4,3,2,1,0:T(8,128)(2,1)}, bf16[1024,4096]{1,0:T(8,128)(2,1)}) custom-call(bf16[256,512]{1,0:T(8,128)(2,1)} %bitcast.20, bf16[1024,4096]{1,0:T(8,128)(2,1)} %own_ref.1), custom_call_target="tpu_custom_call" | custom-call | tf_op jit(solution)/shard_map/pallas_call | solution.py:172
  77.2 0.0 collective-permute-done
  77.2 0.0 copy-done
  77.2 0.1 iota_add_fusion
  77.3 0.4 convert_reduce_fusion
  77.6 0.2 select_reduce_fusion.3
  77.8 0.1 select_reduce_fusion.order_ref
  78.0 0.1 copy.6
  78.1 0.1 reshape.131.slot_ref
  78.2 31.1 %shard_map.38.t_ref = bf16[4,4,4,128,1024]{4,3,2,1,0:T(8,128)(2,1)} custom-call(s32[16]{0:T(128)S(1)} %get-tuple-element.13.count_ref, s32[64]{0:T(128)S(1)} %reshape.131.slot_ref, s32[16]{0:T(128)S(1)} %select_reduce_fusion.order_ref, bf16[1024,4096]{1,0:T(8,128)(2,1)} %own_ref.1, bf16[1024,4096]{1,0:T(8,128)(2,1)} %get-tuple-element.7.other_ref, ...), custom_call_target="tpu_custom_call" | custom-call | flops 4294967296 | bytes 50331648 | tf_op jit(solution)/shard_map/pallas_call | solution.py:287
  109.3 116.0 %shard_map.39 = bf16[256,4096]{1,0:T(8,128)(2,1)} custom-call(bf16[4,4,4,128,1024]{4,3,2,1,0:T(8,128)(2,1)} %shard_map.38.t_ref, bf16[4,4,4,128,1024]{4,3,2,1,0:T(8,128)(2,1)} %get-tuple-element.8.s_ref.basis_ref, bf16[256,512]{1,0:T(8,128)(2,1)} %bitcast.21), custom_call_target="tpu_custom_call" | custom-call | tf_op jit(solution)/shard_map/pallas_call | solution.py:575
  225.3 3.1 %copy.8 = bf16[1,256,4096]{2,1,0:T(8,128)(2,1)} copy(bf16[1,256,4096]{2,1,0:T(8,128)(2,1)} %bitcast.19) | data formatting | bytes 4194304
  (4 shorter events, 0.0 us)
Async XLA Ops:
  0.0 77.2 %copy-start = (s32[8,1]{0,1:T(1,128)S(1)}, s32[8,1]{0,1:T(1,128)}, u32[]{:S(2)}) copy-start(s32[8,1]{0,1:T(1,128)} %param.4) | copy-start | bytes 100
  0.0 77.2 %collective-permute-start = (s32[8]{0:T(128)}, s32[8]{0:T(128)S(1)}, u32[]{:S(2)}, u32[]{:S(2)}) collective-permute-start(s32[8]{0:T(128)} %bitcast.23), channel_id=1, source_target_pairs={{0,16},{16,0},{32,48},{48,32},{64,80},{80,64},{96,112},{112,96},{1... | collective-permute-start | bytes 104 | tf_op jit(solution)/shard_map/ppermute | solution.py:618

commit v4 on v3

v4 whole, which is shorter than its diff:
```python
import functools

import jax
import jax.numpy as jnp
from jax import lax
from jax.experimental import pallas as pl
from jax.experimental.pallas import tpu as pltpu
from jax.sharding import PartitionSpec as P

D = 4096
L = 256
BLOCK = 128
NBLK = 8
EXPERTS = 16
ITERS = 5
N_DP = 8
COLS = D // N_DP
QUARTER = D // 4
HALF = L // 2
EPSILON = 1e-06
HIGHEST = lax.Precision.HIGHEST
MESH = pl.DeviceIdType.MESH
RING = 4
ORDERS = ((0, 1, 2), (1, 2, 0), (2, 0, 1))


def mm_nt(a, b):
    return lax.dot_general(a, b, (((1,), (1,)), ((), ())), preferred_element_type=jnp.float32)


def position():
    dp, expert = lax.axis_index("dp"), lax.axis_index("expert")
    return (dp // 2, expert // 4, lax.rem(expert, 4)), lax.rem(dp, 2)


def device(coords, core):
    return (2 * coords[0] + core, 4 * coords[1] + coords[2])


def moved(coords, axis, by):
    return tuple(lax.rem(c + by, RING) if k == axis else c for k, c in enumerate(coords))


def meet(coords, core):
    barrier = pltpu.get_barrier_semaphore()
    peers = [device(moved(coords, a, by), core) for a in range(3) for by in (1, 3)]
    peers.append(device(coords, 1 - core))
    for peer in peers:
        pl.semaphore_signal(barrier, inc=1, device_id=peer, device_id_type=MESH)
    pl.semaphore_wait(barrier, len(peers))


PIECES = tuple((32 * k, 32, 0, QUARTER, ORDERS[k], True) for k in range(3)) + tuple(
    (96, 32, first, count, ORDERS[k], False)
    for k, (first, count) in enumerate(((0, 384), (384, 384), (768, 256)))
)
GATHER_COPIES = 4 * sum(6 if piece[5] else 3 for piece in PIECES)
ALL = slice(None)


class GatherRing:
    def __init__(self, env, piece, fixed, axis):
        self.env, self.piece, self.fixed, self.axis = env, piece, fixed, axis
        self.ids = [env["count"] + k for k in range(4)]
        env["count"] += 4

    def view(self, shift, half=None):
        coords = self.env["coords"]
        row, rows, col, cols = self.piece[:4]
        if half is not None:
            row, rows = row + half * (rows // 2), rows // 2
        index = []
        for axis in range(3):
            step = shift if axis == self.axis else self.fixed.get(axis, 0)
            index.append(ALL if step is ALL else pl.ds(lax.rem(coords[axis] + step, RING), 1))
        return self.env["ref"].at[(*index, pl.ds(row, rows), pl.ds(col, cols))]

    def push(self, which, ref, by):
        env, k = self.env, self.ids[which]
        target = device(moved(env["coords"], self.axis, by), env["core"])
        copy = pltpu.make_async_remote_copy(
            ref, ref, env["send"].at[k], env["recv"].at[k], target, MESH
        )
        copy.start()
        env["sent"].append(copy)

    def arrived(self, which, ref):
        pltpu.make_async_copy(ref, ref, self.env["recv"].at[self.ids[which]]).wait()

    def start(self):
        self.push(0, self.view(0), 1)
        self.push(1, self.view(0), 3)

    def forward(self):
        self.arrived(0, self.view(3))
        self.push(2, self.view(3, 0), 1)
        self.arrived(1, self.view(1))
        self.push(3, self.view(1, 1), 3)

    def finish(self):
        self.arrived(2, self.view(2, 0))
        self.arrived(3, self.view(2, 1))


def gather_kernel(sketch_ref, grads_ref, basis_ref, other_ref, send, recv, pair_send, pair_recv, local):
    coords, core = position()
    meet(coords, core)
    partner = device(coords, 1 - core)
    cols = pl.ds(pl.multiple_of(core * COLS, COLS), COLS)
    own_rows = pl.ds(pl.multiple_of(core * HALF, HALF), HALF)
    other_rows = pl.ds(pl.multiple_of((1 - core) * HALF, HALF), HALF)
    spot = basis_ref.at[coords[0], coords[1], coords[2], :, cols]
    keep = pltpu.make_async_copy(sketch_ref.at[own_rows], spot, local)
    keep.start()
    give = pltpu.make_async_remote_copy(
        sketch_ref.at[other_rows], spot, pair_send.at[0], pair_recv.at[0], partner, MESH
    )
    give.start()
    swap = pltpu.make_async_remote_copy(
        grads_ref, other_ref, pair_send.at[1], pair_recv.at[1], partner, MESH
    )
    keep.wait()
    give.wait()

    env = dict(coords=coords, core=core, ref=basis_ref, send=send, recv=recv, sent=[], count=0)
    first, second, third = [], [], []
    for piece in PIECES:
        a1, a2, a3 = piece[4]
        first.append(GatherRing(env, piece, {}, a1))
        second.append(GatherRing(env, piece, {a1: ALL}, a2))
        steps = (0, 3, 1, 2) if piece[5] else (ALL,)
        third.append([GatherRing(env, piece, {a1: ALL, a2: k}, a3) for k in steps])
    sliced = [k for k, piece in enumerate(PIECES) if piece[5]]
    for ring in first:
        ring.start()
    swap.start()
    for ring in first:
        ring.forward()
    for k, ring in enumerate(first):
        ring.finish()
        second[k].start()
    for k in sliced:
        third[k][0].start()
    for ring in second:
        ring.forward()
    for k in sliced:
        third[k][1].start()
        third[k][2].start()
    for k in sliced:
        third[k][0].forward()
    for k, ring in enumerate(second):
        ring.finish()
        third[k][-1].start()
    for step in (1, 2, 3):
        for k in sliced:
            third[k][step].forward()
    for k in range(len(PIECES)):
        if k not in sliced:
            third[k][0].forward()
    for rings in third:
        for ring in rings:
            ring.finish()
    for copy in env["sent"]:
        copy.wait_send()
    swap.wait()


def gather(sketch, grads):
    return pl.pallas_call(
        gather_kernel,
        out_shape=(
            jax.ShapeDtypeStruct((4, 4, 4, HALF, QUARTER), jnp.bfloat16),
            jax.ShapeDtypeStruct(grads.shape, jnp.bfloat16),
        ),
        in_specs=[
            pl.BlockSpec(memory_space=pltpu.VMEM),
            pl.BlockSpec(memory_space=pl.ANY),
        ],
        out_specs=(pl.BlockSpec(memory_space=pl.ANY), pl.BlockSpec(memory_space=pl.ANY)),
        scratch_shapes=[
            pltpu.SemaphoreType.DMA((GATHER_COPIES,)),
            pltpu.SemaphoreType.DMA((GATHER_COPIES,)),
            pltpu.SemaphoreType.DMA((2,)),
            pltpu.SemaphoreType.DMA((2,)),
            pltpu.SemaphoreType.DMA,
        ],
        compiler_params=pltpu.CompilerParams(collective_id=0, has_side_effects=True),
    )(sketch, grads)


def slot_table(owners):
    ids = jnp.arange(EXPERTS, dtype=jnp.int32)
    hit = owners[None, :] == ids[:, None]
    count = jnp.sum(hit.astype(jnp.int32), axis=1)
    blocks = owners.shape[0]
    b = jnp.arange(blocks, dtype=jnp.int32)
    rank = jnp.sum(hit[:, None, :] & (b[None, :] < b[:, None])[None], axis=2).astype(jnp.int32)
    slot0 = jnp.sum(jnp.where(hit & (rank == 0), b[None, :], 0), axis=1)
    slots = [
        jnp.where(count > j, jnp.sum(jnp.where(hit & (rank == j), b[None, :], 0), axis=1), slot0)
        for j in range(4)
    ]
    return count, jnp.stack(slots, axis=1).reshape(-1)


class ReduceRing:
    def __init__(self, env, axis, lead, held, far, near, store):
        self.env, self.axis, self.lead = env, axis, lead
        self.held, self.far, self.near, self.store = held, far, near, store
        self.ids = [env["count"] + k for k in range(6)]
        env["count"] += 6

    def push(self, which, src, dst, by):
        env, k = self.env, self.ids[which]
        target = device(moved(env["coords"], self.axis, by), env["core"])
        copy = pltpu.make_async_remote_copy(
            src, dst, env["send"].at[k], env["recv"].at[k], target, MESH
        )
        copy.start()
        env["sent"].append(copy)

    def arrived(self, which, ref):
        pltpu.make_async_copy(ref, ref, self.env["recv"].at[self.ids[which]]).wait()

    def each(self, fn):
        if self.lead == 0:
            fn(())
            return

        def body(i, carry):
            fn((i,) if self.lead == 1 else (lax.div(i, RING), lax.rem(i, RING)))
            return carry

        lax.fori_loop(0, RING**self.lead, body, 0)

    def send_far(self):
        self.push(0, self.held(2, 0), self.far.at[0], 1)
        self.push(1, self.held(2, 1), self.far.at[1], 3)

    def send_right(self):
        self.push(2, self.held(1, 1), self.near.at[1], 1)

    def send_left(self):
        self.push(3, self.held(3, 0), self.near.at[2], 3)

    def begin(self):
        self.send_far()
        self.send_right()
        self.send_left()

    def forward_half(self, half):
        shift, dst = ((1, 0), (3, 3))[half]
        self.arrived(half, self.far.at[half])
        mine, far = self.held(shift, half), self.far

        def add(index):
            total = far[(half, *index)].astype(jnp.float32) + mine[index].astype(jnp.float32)
            far[(half, *index)] = total.astype(far.dtype)

        self.each(add)
        self.push(4 + half, far.at[half], self.near.at[dst], shift)

    def forward(self):
        self.forward_half(0)
        self.forward_half(1)

    def finish(self):
        near = self.near
        for which, slot in ((2, 1), (3, 2), (4, 0), (5, 3)):
            self.arrived(which, near.at[slot])
        for half in range(2):
            mine = self.held(0, half)

            def add(index, half=half, mine=mine):
                total = mine[index].astype(jnp.float32) + near[(half, *index)].astype(jnp.float32)
                self.store(half, index, total + near[(2 + half, *index)].astype(jnp.float32))

            self.each(add)


PARTS = ((0, 48), (48, 48), (96, 32))
AXES = ((0, 2, 1), (1, 2, 0), (2, 0, 1))
REDUCE_COPIES = 6 * (4 + 4 + 1 + 2 * 3)


def cols_of_half(half):
    return pl.ds(half * COLS, COLS)


def reduce_buffers():
    b16, f32 = jnp.bfloat16, jnp.float32
    shapes = {
        "g": pltpu.VMEM((2 * NBLK, BLOCK, D), b16),
        "s": pltpu.VMEM((2, 4, HALF, QUARTER), b16),
        "p": pltpu.VMEM((HALF, 4 * BLOCK), b16),
        "t": pltpu.VMEM((4, 4, 4, HALF, QUARTER), b16),
    }
    for k, (_, rows) in enumerate(PARTS):
        lead = (4, 4) if k == 2 else (4,)
        slices = 1 if k == 2 else 4
        shapes["far1", k] = pltpu.VMEM((slices, 2, *lead, rows, COLS), b16)
        shapes["near1", k] = pltpu.VMEM((slices, 4, *lead, rows, COLS), b16)
        shapes["far2", k] = pltpu.VMEM((2, 4, rows, COLS), b16)
        shapes["near2", k] = pltpu.VMEM((4, 4, rows, COLS), b16)
        shapes["sum2", k] = pltpu.VMEM((4, rows, QUARTER), f32)
        shapes["far3", k] = pltpu.VMEM((2, rows, COLS), f32)
        shapes["near3", k] = pltpu.VMEM((4, rows, COLS), f32)
    shapes["final"] = pltpu.VMEM((HALF, QUARTER), f32)
    shapes["whole"] = pltpu.VMEM((2, 4, HALF, QUARTER), b16)
    shapes["term"] = pltpu.VMEM((L, COLS), f32)
    shapes["gp"] = pltpu.VMEM((L, L), f32)
    shapes["gin"] = pltpu.VMEM((HALF, L), f32)
    shapes["gx"] = pltpu.VMEM((3, HALF, L), f32)
    shapes["gfull"] = pltpu.VMEM((L, L), f32)
    for name, count in (
        ("send", REDUCE_COPIES), ("recv", REDUCE_COPIES), ("load", 5),
        ("pair_send", 9), ("pair_recv", 9), ("x_send", 10), ("x_recv", 10),
    ):
        shapes[name] = pltpu.SemaphoreType.DMA((count,))
    return shapes


def reduce_kernel(
    names, count_ref, slot_ref, grads_ref, other_ref, basis_ref, sketch_ref, out_ref, *scratch
):
    buf = dict(zip(names, scratch))
    coords, core = position()
    final, whole, term, gp, gin, gx, gfull = (
        buf[k] for k in ("final", "whole", "term", "gp", "gin", "gx", "gfull")
    )
    pair_send, pair_recv, x_send, x_recv = (
        buf[k] for k in ("pair_send", "pair_recv", "x_send", "x_recv")
    )
    g_ref, s_ref, p_ref, t_ref, load = (buf[k] for k in ("g", "s", "p", "t", "load"))
    env = dict(coords=coords, core=core, send=buf["send"], recv=buf["recv"], sent=[], count=0)

    def at(axis, shift):
        return lax.rem(coords[axis] + shift, RING)

    steps = (2, 1, 3, 0)
    grads_in = [
        pltpu.make_async_copy(grads_ref, g_ref.at[0:NBLK], load.at[0]),
        pltpu.make_async_copy(other_ref, g_ref.at[NBLK : 2 * NBLK], load.at[1]),
    ]

    def basis_in(y, z, slot):
        return pltpu.make_async_copy(basis_ref.at[:, y, z], s_ref.at[slot], load.at[2 + slot])

    def compute(turn):
        step = steps[turn]
        z = at(2, step)

        def body(y, carry):
            slot = lax.rem(y, 2)
            basis_in(y, z, slot).wait()

            @pl.when(y < 3)
            def _():
                basis_in(y + 1, z, 1 - slot).start()

            e = 4 * y + z
            blocks = [slot_ref[4 * e + j] for j in range(4)]

            def rows(lo, hi):
                return jnp.concatenate([g_ref[b, :, lo:hi] for b in blocks], axis=0)

            acc = mm_nt(rows(0, QUARTER), s_ref[slot, 0])
            for x in range(1, 4):
                acc += mm_nt(rows(x * QUARTER, (x + 1) * QUARTER), s_ref[slot, x])
            place = lax.broadcasted_iota(jnp.int32, acc.shape, 0) // BLOCK
            p_ref[...] = jnp.where(place < count_ref[e], acc, 0.0).T.astype(jnp.bfloat16)
            for c in range(N_DP):
                value = mm(p_ref[...], rows(c * COLS, (c + 1) * COLS))
                t_ref[step, y, c // 2, :, (c % 2) * COLS : (c % 2 + 1) * COLS] = value.astype(
                    jnp.bfloat16
                )
            return carry

        lax.fori_loop(0, 4, body, 0)
        if turn < 3:
            basis_in(0, at(2, steps[turn + 1]), 0).start()

    def first_ring(k, slot, step):
        row, count = PARTS[k]
        rows = pl.ds(row, count)

        def held(shift, half):
            cols = cols_of_half(half)
            if k == 0:
                return t_ref.at[step, :, at(0, shift), rows, cols]
            if k == 1:
                return t_ref.at[step, at(1, shift), :, rows, cols]
            return t_ref.at[shift, :, :, rows, cols]

        def store(half, index, value):
            if k == 0:
                place = (step, index[0], coords[0])
            elif k == 1:
                place = (step, coords[1], index[0])
            else:
                place = (0, *index)
            t_ref[(*place, rows, cols_of_half(half))] = value.astype(jnp.bfloat16)

        far, near = buf["far1", k].at[slot], buf["near1", k].at[slot]
        return ReduceRing(env, k, 2 if k == 2 else 1, held, far, near, store)

    def second_ring(k):
        row, count = PARTS[k]
        rows = pl.ds(row, count)
        out = buf["sum2", k]

        def held(shift, half):
            cols = cols_of_half(half)
            if k == 0:
                return t_ref.at[shift, :, coords[0], rows, cols]
            if k == 1:
                return t_ref.at[shift, coords[1], :, rows, cols]
            return t_ref.at[0, :, at(0, shift), rows, cols]

        def store(half, index, value):
            out[(*index, ALL, cols_of_half(half))] = value

        return ReduceRing(env, AXES[k][1], 1, held, buf["far2", k], buf["near2", k], store)

    def third_ring(k):
        row, count = PARTS[k]
        axis = AXES[k][2]

        def held(shift, half):
            return buf["sum2", k].at[at(axis, shift), :, cols_of_half(half)]

        def store(half, index, value):
            final[row : row + count, half * COLS : (half + 1) * COLS] = value

        return ReduceRing(env, axis, 0, held, buf["far3", k], buf["near3", k], store)

    sliced = {
        step: [first_ring(k, slot, step) for k in range(2)] for slot, step in enumerate(steps)
    }
    deep = first_ring(2, 0, None)
    second = [second_ring(k) for k in range(3)]
    third = [third_ring(k) for k in range(3)]

    for c in grads_in:
        c.start()
    basis_in(0, at(2, steps[0]), 0).start()
    whole_own = pltpu.make_async_copy(
        basis_ref.at[:, coords[1], coords[2]], whole.at[core], load.at[4]
    )
    meet(coords, core)
    for c in grads_in:
        c.wait()

    def run(rings, method):
        for ring in rings:
            method(ring)

    begin, forward, finish = ReduceRing.begin, ReduceRing.forward, ReduceRing.finish
    compute(0)
    run(sliced[2], begin)
    deep.send_far()
    compute(1)
    run(sliced[1], begin)
    deep.send_right()
    run(sliced[2], forward)
    deep.forward_half(0)
    compute(2)
    run(sliced[3], begin)
    deep.send_left()
    deep.forward_half(1)
    run(sliced[1], forward)
    whole_own.start()
    whole_swap = pltpu.make_async_remote_copy(
        basis_ref.at[:, coords[1], coords[2]],
        whole.at[core],
        pair_send.at[8],
        pair_recv.at[8],
        device(coords, 1 - core),
        MESH,
    )
    whole_swap.start()
    run(sliced[2], finish)
    run(second[:2], ReduceRing.send_far)
    compute(3)
    run(sliced[0], begin)
    run(sliced[3], forward)
    run(sliced[1], finish)
    run(second[:2], ReduceRing.send_right)
    deep.finish()
    second[2].begin()
    run(sliced[0], forward)
    run(sliced[3], finish)
    run(second[:2], ReduceRing.send_left)
    whole_own.wait()
    whole_swap.wait()
    gp[...] = jnp.zeros_like(gp)
    for x in range(4):
        for h in range(2):
            gp[h * HALF : (h + 1) * HALF, 0:HALF] += mm_nt(whole[h, x], whole[0, x])
            gp[h * HALF : (h + 1) * HALF, HALF:] += mm_nt(whole[h, x], whole[1, x])
    run(second, forward)
    run(sliced[0], finish)
    for k in (2, 0, 1):
        second[k].finish()
        third[k].begin()
    for k in (2, 0, 1):
        third[k].forward()
    run(third, finish)
    sent = env["sent"]
    partner = device(coords, 1 - core)
    mine = pl.ds(pl.multiple_of(core * HALF, HALF), HALF)
    theirs = pl.ds(pl.multiple_of((1 - core) * HALF, HALF), HALF)

    def give(src, dst, which):
        c = pltpu.make_async_remote_copy(
            src, dst, pair_send.at[which], pair_recv.at[which], partner, MESH
        )
        c.start()
        return c

    def across(src, dst, which, by):
        c = pltpu.make_async_remote_copy(
            src, dst, x_send.at[which], x_recv.at[which], device(moved(coords, 0, by), core), MESH
        )
        c.start()
        return c

    here = pl.ds(pl.multiple_of(core * COLS, COLS), COLS)
    there = pl.ds(pl.multiple_of((1 - core) * COLS, COLS), COLS)
    swap = give(final.at[:, there], term.at[mine], 0)
    term[mine, :] = final[:, here]
    product = two_pass(gp[...], sketch_ref[...])
    swap.wait()
    average = float(BLOCK * NBLK * N_DP)
    unscaled = product + term[...] / average
    term[...] = unscaled
    gp[...] = three_pass_nt(unscaled, unscaled)
    swap = give(gp.at[theirs], gin, 1)
    swap.wait()
    gin[...] = gin[...] + gp[mine, :]
    quarter = HALF // 2
    right = across(gin, gx.at[0], 0, 1)
    left = across(gin, gx.at[1], 1, 3)
    right.wait_recv()
    on_right = across(gx.at[0, 0:quarter], gx.at[2, 0:quarter], 2, 1)
    left.wait_recv()
    on_left = across(gx.at[1, quarter:HALF], gx.at[2, quarter:HALF], 3, 3)
    for c in (right, left):
        c.wait_send()
    on_right.wait()
    on_left.wait()
    gfull[mine, :] = (gin[...] + gx[2]) + (gx[0] + gx[1])
    swap = give(gfull.at[mine], gfull.at[mine], 2)
    swap.wait()
    gram = gfull[...]
    row = lax.broadcasted_iota(jnp.int32, (L, L), 0)
    col = lax.broadcasted_iota(jnp.int32, (L, L), 1)
    diagonal = row == col
    total = jnp.sum(jnp.where(diagonal, gram, 0.0)) + EPSILON
    total = jnp.full((1, 1), total, jnp.float32)
    a = gram / total
    q = None
    for step in range(ITERS):
        p = jnp.where(diagonal, 1.5, 0.0) - 0.5 * a
        q = p if q is None else three_pass(p, q)
        if step < ITERS - 1:
            a = three_pass(three_pass(p, a), p)
    scale = D**0.5 * lax.rsqrt(total)
    factor = three_pass(q, term[...] * scale)

    def chunk(shift, core_of):
        index = 2 * lax.rem(coords[0] + shift, RING) + core_of
        return pl.ds(pl.multiple_of(index * COLS, COLS), COLS)

    def piece(shift, rows=slice(None)):
        return out_ref.at[rows, chunk(shift, core)]

    out_ref[:, chunk(0, core)] = factor.astype(jnp.bfloat16)
    upper, lower = pl.ds(0, HALF), pl.ds(HALF, HALF)
    right = across(piece(0, upper), piece(0, upper), 4, 1)
    left = across(piece(0, lower), piece(0, lower), 6, 3)
    right_rest = across(piece(0, lower), piece(0, lower), 5, 1)
    left_rest = across(piece(0, upper), piece(0, upper), 7, 3)
    gives = [give(piece(0), piece(0), 3)]
    right.wait_recv()
    on_right = across(piece(3, upper), piece(3, upper), 8, 1)
    left.wait_recv()
    on_left = across(piece(1, lower), piece(1, lower), 9, 3)
    right_rest.wait_recv()
    gives.append(give(piece(3), piece(3), 4))
    left_rest.wait_recv()
    gives.append(give(piece(1), piece(1), 5))
    on_right.wait_recv()
    gives.append(give(piece(2, upper), piece(2, upper), 6))
    on_left.wait_recv()
    gives.append(give(piece(2, lower), piece(2, lower), 7))
    for c in (right, left, right_rest, left_rest, on_right, on_left):
        c.wait_send()
    for c in gives:
        c.wait()
    for c in sent:
        c.wait_send()


def split(a):
    high = a.astype(jnp.bfloat16)
    return high, (a - high.astype(jnp.float32)).astype(jnp.bfloat16)


def mm(a, b):
    return jnp.dot(a, b, preferred_element_type=jnp.float32)


def two_pass(a, b):
    high, low = split(a)
    return mm(high, b) + mm(low, b)


def three_pass(a, b):
    ah, al = split(a)
    bh, bl = split(b)
    return mm(ah, bh) + (mm(ah, bl) + mm(al, bh))


def three_pass_nt(a, b):
    ah, al = split(a)
    bh, bl = split(b)
    return mm_nt(ah, bh) + (mm_nt(ah, bl) + mm_nt(al, bh))


def reduce_terms(count, slots, grads, other, basis, own):
    buffers = reduce_buffers()
    smem, vmem, where = (
        pl.BlockSpec(memory_space=m) for m in (pltpu.SMEM, pltpu.VMEM, pl.ANY)
    )
    return pl.pallas_call(
        functools.partial(reduce_kernel, tuple(buffers)),
        out_shape=jax.ShapeDtypeStruct((L, D), jnp.bfloat16),
        in_specs=[smem, smem, where, where, where, vmem],
        out_specs=vmem,
        scratch_shapes=list(buffers.values()),
        compiler_params=pltpu.CompilerParams(
            collective_id=1, has_side_effects=True, vmem_limit_bytes=67043328
        ),
    )(count, slots, grads, other, basis, own)


def shards(grads, block_expert, sketch):
    own = sketch[0]
    owners = block_expert[:, 0]
    theirs = lax.ppermute(owners, "dp", [(k, k ^ 1) for k in range(N_DP)])
    grads = grads.reshape(NBLK, BLOCK, D)
    basis, other = gather(own, grads)
    count, slots = slot_table(jnp.concatenate([owners, theirs]))
    return reduce_terms(count, slots, grads, other, basis, own)[None]


def solution(mesh):
    in_specs = (P(("dp", "expert"), None), P(("dp", "expert"), None), P("expert", None, "dp"))
    out_specs = P("expert", None, None)
    return jax.shard_map(shards, mesh=mesh, in_specs=in_specs, out_specs=out_specs, check_vma=False)
```

time: 229 us -> 219 us (0.956)
  Pallas kernels: 223 us -> 212 us
    pallas_call x2 -> x1, Pallas kernels: 147 us -> 136 us  [reduce_terms(): pl.pallas_call(functools.partial(reduce_kernel, tuple(buffers)), out_shap...]
  transfers between devices with their start and end apart: 1 -> 1, of which waited for: 0 -> 0; matrix products, arithmetic and copies ran while one was open for 0% -> 0% of each run, Pallas kernels for 33% -> 35%
where the time goes in v4:
time: 219 us; the launch traced here: 218 us
  Pallas kernels  212 us (97%)
  local copies, waits for them, and re-layouts  4.29 us (2%)
    pallas_call x1, Pallas kernels, reduce_terms(): pl.pallas_call(functools.partial(reduce_kernel, tuple(buffers)), out_shap...  136 us
    pallas_call x1, Pallas kernels, gather(): pl.pallas_call(gather_kernel, out_shape=(jax.ShapeDtypeStruct((4, 4, 4, H...  75.8 us
  transfers between devices with their start and end apart: 1, of which 0 were waited for; matrix products, arithmetic and copies ran while one was open for 0% of the time, Pallas kernels for 35%

profile of v4, /device:TPU:1, one launch (start us, length us, event | category | flops | bytes accessed | tf_op | source)
XLA Modules:
  0.0 218.5 jit_solution(3849999377581641739)
XLA Ops:
  0.0 0.0 copy-start.1
  0.0 1.4 collective-permute-start
  1.4 75.8 %shard_map.37 = (bf16[4,4,4,128,1024]{4,3,2,1,0:T(8,128)(2,1)}, bf16[8,128,4096]{2,1,0:T(8,128)(2,1)}) custom-call(bf16[256,512]{1,0:T(8,128)(2,1)} %bitcast.23, bf16[8,128,4096]{2,1,0:T(8,128)(2,1)} %bitcast.20), custom_call_target="tpu_custom_call" | custom-call | tf_op jit(solution)/shard_map/pallas_call | solution.py:169
  77.2 0.0 collective-permute-done
  77.2 0.0 copy-done.1
  77.2 0.1 pad_add_fusion.1
  77.3 0.4 convert_reduce_fusion
  77.6 0.2 select_reduce_fusion.2
  77.8 0.0 copy-start
  77.8 0.5 copy-done
  78.3 0.1 copy.6
  78.4 0.6 reshape.94.slot_ref
  79.0 136.4 %shard_map.38 = bf16[256,4096]{1,0:T(8,128)(2,1)} custom-call(s32[16]{0:T(128)} %copy-done, s32[64]{0:T(128)} %reshape.94.slot_ref, bf16[8,128,4096]{2,1,0:T(8,128)(2,1)} %bitcast.21, bf16[8,128,4096]{2,1,0:T(8,128)(2,1)} %get-tuple-element.7.other_ref, bf16[4,4,4,128,1024]{4,3,2,1,0:T(8,128)(2,1)} %get-tuple-element.8.basis_ref, bf16[256,512]{1,0:T(8,128)(2,1)} %bitcast.24), custom_call_target="tpu_custom_call" | custom-call | tf_op jit(solution)/shard_map/pallas_call | solution.py:636
  215.4 3.1 %copy.8 = bf16[1,256,4096]{2,1,0:T(8,128)(2,1)} copy(bf16[1,256,4096]{2,1,0:T(8,128)(2,1)} %bitcast.22) | data formatting | bytes 4194304
  (4 shorter events, 0.0 us)
Async XLA Ops:
  0.0 77.2 %copy-start.1 = (s32[8,1]{0,1:T(1,128)S(1)}, s32[8,1]{0,1:T(1,128)}, u32[]{:S(2)}) copy-start(s32[8,1]{0,1:T(1,128)} %param.4) | copy-start | bytes 100
  0.0 77.2 %collective-permute-start = (s32[8]{0:T(128)}, s32[8]{0:T(128)S(1)}, u32[]{:S(2)}, u32[]{:S(2)}) collective-permute-start(s32[8]{0:T(128)} %bitcast.26), channel_id=1, source_target_pairs={{0,16},{16,0},{32,48},{48,32},{64,80},{80,64},{96,112},{112,96},{1... | collective-permute-start | bytes 104 | tf_op jit(solution)/shard_map/ppermute | solution.py:651
  77.8 0.5 copy-start

commit v5 on v4

--- a/solution.py
+++ b/solution.py
@@ -1,4 +1,5 @@
 import functools
+import math
 
 import jax
 import jax.numpy as jnp
@@ -54,7 +55,7 @@
     (96, 32, first, count, ORDERS[k], False)
     for k, (first, count) in enumerate(((0, 384), (384, 384), (768, 256)))
 )
-GATHER_COPIES = 4 * sum(6 if piece[5] else 3 for piece in PIECES)
+GATHER_COPIES = 4 * sum(9 if piece[5] else 3 for piece in PIECES)
 ALL = slice(None)
 
 
@@ -127,29 +128,40 @@
     for piece in PIECES:
         a1, a2, a3 = piece[4]
         first.append(GatherRing(env, piece, {}, a1))
-        second.append(GatherRing(env, piece, {a1: ALL}, a2))
         steps = (0, 3, 1, 2) if piece[5] else (ALL,)
+        second.append([GatherRing(env, piece, {a1: k}, a2) for k in steps])
         third.append([GatherRing(env, piece, {a1: ALL, a2: k}, a3) for k in steps])
     sliced = [k for k, piece in enumerate(PIECES) if piece[5]]
     for ring in first:
         ring.start()
+    for k in sliced:
+        second[k][0].start()
     swap.start()
-    for ring in first:
+    for k, ring in enumerate(first):
         ring.forward()
+        if k in sliced:
+            second[k][1].start()
+            second[k][2].start()
+    for k in sliced:
+        second[k][0].forward()
     for k, ring in enumerate(first):
         ring.finish()
-        second[k].start()
+        second[k][-1].start()
     for k in sliced:
         third[k][0].start()
-    for ring in second:
-        ring.forward()
+    for step in (1, 2):
+        for k in sliced:
+            second[k][step].forward()
+    for rings in second:
+        rings[-1].forward()
     for k in sliced:
         third[k][1].start()
         third[k][2].start()
     for k in sliced:
         third[k][0].forward()
-    for k, ring in enumerate(second):
-        ring.finish()
+    for k, rings in enumerate(second):
+        for ring in rings:
+            ring.finish()
         third[k][-1].start()
     for step in (1, 2, 3):
         for k in sliced:
@@ -223,15 +235,15 @@
         pltpu.make_async_copy(ref, ref, self.env["recv"].at[self.ids[which]]).wait()
 
     def each(self, fn):
-        if self.lead == 0:
+        if not self.lead:
             fn(())
             return
 
         def body(i, carry):
-            fn((i,) if self.lead == 1 else (lax.div(i, RING), lax.rem(i, RING)))
+            fn((i,) if len(self.lead) == 1 else (lax.div(i, RING), lax.rem(i, RING)))
             return carry
 
-        lax.fori_loop(0, RING**self.lead, body, 0)
+        lax.fori_loop(0, math.prod(self.lead), body, 0)
 
     def send_far(self):
         self.push(0, self.held(2, 0), self.far.at[0], 1)
@@ -280,7 +292,9 @@
 
 PARTS = ((0, 48), (48, 48), (96, 32))
 AXES = ((0, 2, 1), (1, 2, 0), (2, 0, 1))
-REDUCE_COPIES = 6 * (4 + 4 + 1 + 2 * 3)
+REDUCE_COPIES = 6 * (8 + 4 + 2 + 2 * 3)
+STEPS = (2, 1, 3, 0)
+PLACE = {2: 0, 1: 1, 3: 2, 0: 3}
 
 
 def cols_of_half(half):
@@ -296,8 +310,7 @@
         "t": pltpu.VMEM((4, 4, 4, HALF, QUARTER), b16),
     }
     for k, (_, rows) in enumerate(PARTS):
-        lead = (4, 4) if k == 2 else (4,)
-        slices = 1 if k == 2 else 4
+        slices, lead = ((8, (2,)), (4, (4,)), (2, (2, 4)))[k]
         shapes["far1", k] = pltpu.VMEM((slices, 2, *lead, rows, COLS), b16)
         shapes["near1", k] = pltpu.VMEM((slices, 4, *lead, rows, COLS), b16)
         shapes["far2", k] = pltpu.VMEM((2, 4, rows, COLS), b16)
@@ -337,7 +350,6 @@
     def at(axis, shift):
         return lax.rem(coords[axis] + shift, RING)
 
-    steps = (2, 1, 3, 0)
     grads_in = [
         pltpu.make_async_copy(grads_ref, g_ref.at[0:NBLK], load.at[0]),
         pltpu.make_async_copy(other_ref, g_ref.at[NBLK : 2 * NBLK], load.at[1]),
@@ -346,17 +358,25 @@
     def basis_in(y, z, slot):
         return pltpu.make_async_copy(basis_ref.at[:, y, z], s_ref.at[slot], load.at[2 + slot])
 
-    def compute(turn):
-        step = steps[turn]
+    def compute(turn, part):
+        step = STEPS[turn]
         z = at(2, step)
-
-        def body(y, carry):
-            slot = lax.rem(y, 2)
-            basis_in(y, z, slot).wait()
-
-            @pl.when(y < 3)
+        shifts = STEPS[2 * part : 2 * part + 2]
+
+        def body(i, carry):
+            y = lax.rem(coords[1] + shifts[0] + i * (shifts[1] - shifts[0]), RING)
+            basis_in(y, z, i).wait()
+
+            @pl.when(i == 0)
             def _():
-                basis_in(y + 1, z, 1 - slot).start()
+                basis_in(at(1, shifts[1]), z, 1).start()
+
+            if turn < 3 or part == 0:
+                z_next = z if part == 0 else at(2, STEPS[turn + 1])
+
+                @pl.when(i == 1)
+                def _():
+                    basis_in(at(1, STEPS[2 - 2 * part]), z_next, 0).start()
 
             e = 4 * y + z
             blocks = [slot_ref[4 * e + j] for j in range(4)]
@@ -364,45 +384,43 @@
             def rows(lo, hi):
                 return jnp.concatenate([g_ref[b, :, lo:hi] for b in blocks], axis=0)
 
-            acc = mm_nt(rows(0, QUARTER), s_ref[slot, 0])
+            acc = mm_nt(rows(0, QUARTER), s_ref[i, 0])
             for x in range(1, 4):
-                acc += mm_nt(rows(x * QUARTER, (x + 1) * QUARTER), s_ref[slot, x])
+                acc += mm_nt(rows(x * QUARTER, (x + 1) * QUARTER), s_ref[i, x])
             place = lax.broadcasted_iota(jnp.int32, acc.shape, 0) // BLOCK
             p_ref[...] = jnp.where(place < count_ref[e], acc, 0.0).T.astype(jnp.bfloat16)
             for c in range(N_DP):
                 value = mm(p_ref[...], rows(c * COLS, (c + 1) * COLS))
-                t_ref[step, y, c // 2, :, (c % 2) * COLS : (c % 2 + 1) * COLS] = value.astype(
-                    jnp.bfloat16
-                )
+                cols = slice((c % 2) * COLS, (c % 2 + 1) * COLS)
+                t_ref[step, 2 * part + i, c // 2, :, cols] = value.astype(jnp.bfloat16)
             return carry
 
-        lax.fori_loop(0, 4, body, 0)
-        if turn < 3:
-            basis_in(0, at(2, steps[turn + 1]), 0).start()
-
-    def first_ring(k, slot, step):
+        lax.fori_loop(0, 2, body, 0)
+
+    def first_ring(k, slot, step, part):
         row, count = PARTS[k]
         rows = pl.ds(row, count)
+        base = 2 * part
 
         def held(shift, half):
             cols = cols_of_half(half)
             if k == 0:
-                return t_ref.at[step, :, at(0, shift), rows, cols]
+                return t_ref.at[step, base : base + 2, at(0, shift), rows, cols]
             if k == 1:
-                return t_ref.at[step, at(1, shift), :, rows, cols]
-            return t_ref.at[shift, :, :, rows, cols]
+                return t_ref.at[step, PLACE[shift], :, rows, cols]
+            return t_ref.at[shift, base : base + 2, :, rows, cols]
 
         def store(half, index, value):
             if k == 0:
-                place = (step, index[0], coords[0])
+                place = (step, base + index[0], coords[0])
             elif k == 1:
-                place = (step, coords[1], index[0])
+                place = (step, PLACE[0], index[0])
             else:
-                place = (0, *index)
+                place = (0, base + index[0], index[1])
             t_ref[(*place, rows, cols_of_half(half))] = value.astype(jnp.bfloat16)
 
         far, near = buf["far1", k].at[slot], buf["near1", k].at[slot]
-        return ReduceRing(env, k, 2 if k == 2 else 1, held, far, near, store)
+        return ReduceRing(env, k, ((2,), (4,), (2, 4))[k], held, far, near, store)
 
     def second_ring(k):
         row, count = PARTS[k]
@@ -414,36 +432,36 @@
             if k == 0:
                 return t_ref.at[shift, :, coords[0], rows, cols]
             if k == 1:
-                return t_ref.at[shift, coords[1], :, rows, cols]
+                return t_ref.at[shift, PLACE[0], :, rows, cols]
             return t_ref.at[0, :, at(0, shift), rows, cols]
 
         def store(half, index, value):
             out[(*index, ALL, cols_of_half(half))] = value
 
-        return ReduceRing(env, AXES[k][1], 1, held, buf["far2", k], buf["near2", k], store)
+        return ReduceRing(env, AXES[k][1], (4,), held, buf["far2", k], buf["near2", k], store)
 
     def third_ring(k):
         row, count = PARTS[k]
         axis = AXES[k][2]
 
         def held(shift, half):
-            return buf["sum2", k].at[at(axis, shift), :, cols_of_half(half)]
+            place = PLACE[shift] if axis == 1 else at(axis, shift)
+            return buf["sum2", k].at[place, :, cols_of_half(half)]
 
         def store(half, index, value):
             final[row : row + count, half * COLS : (half + 1) * COLS] = value
 
-        return ReduceRing(env, axis, 0, held, buf["far3", k], buf["near3", k], store)
-
-    sliced = {
-        step: [first_ring(k, slot, step) for k in range(2)] for slot, step in enumerate(steps)
-    }
-    deep = first_ring(2, 0, None)
+        return ReduceRing(env, axis, (), held, buf["far3", k], buf["near3", k], store)
+
+    xs = [[first_ring(0, 2 * t + h, STEPS[t], h) for h in range(2)] for t in range(4)]
+    ys = [first_ring(1, t, STEPS[t], 0) for t in range(4)]
+    zs = [first_ring(2, h, None, h) for h in range(2)]
     second = [second_ring(k) for k in range(3)]
     third = [third_ring(k) for k in range(3)]
 
     for c in grads_in:
         c.start()
-    basis_in(0, at(2, steps[0]), 0).start()
+    basis_in(at(1, STEPS[0]), at(2, STEPS[0]), 0).start()
     whole_own = pltpu.make_async_copy(
         basis_ref.at[:, coords[1], coords[2]], whole.at[core], load.at[4]
     )
@@ -455,20 +473,29 @@
         for ring in rings:
             method(ring)
 
-    begin, forward, finish = ReduceRing.begin, ReduceRing.forward, ReduceRing.finish
-    compute(0)
-    run(sliced[2], begin)
-    deep.send_far()
-    compute(1)
-    run(sliced[1], begin)
-    deep.send_right()
-    run(sliced[2], forward)
-    deep.forward_half(0)
-    compute(2)
-    run(sliced[3], begin)
-    deep.send_left()
-    deep.forward_half(1)
-    run(sliced[1], forward)
+    def batch(turn, part):
+        compute(turn, part)
+        xs[turn][part].begin()
+        if part == 0:
+            ys[turn].send_far()
+            ys[turn].send_right()
+        else:
+            ys[turn].send_left()
+        if turn < 3:
+            (ReduceRing.send_far, ReduceRing.send_right, ReduceRing.send_left)[turn](zs[part])
+
+    forward, finish = ReduceRing.forward, ReduceRing.finish
+    batch(0, 0)
+    batch(0, 1)
+    batch(1, 0)
+    xs[0][0].forward()
+    batch(1, 1)
+    xs[0][1].forward()
+    ys[0].forward()
+    zs[0].forward_half(0)
+    batch(2, 0)
+    zs[1].forward_half(0)
+    xs[1][0].forward()
     whole_own.start()
     whole_swap = pltpu.make_async_remote_copy(
         basis_ref.at[:, coords[1], coords[2]],
@@ -479,17 +506,28 @@
         MESH,
     )
     whole_swap.start()
-    run(sliced[2], finish)
+    batch(2, 1)
+    zs[0].forward_half(1)
+    xs[1][1].forward()
+    ys[1].forward()
+    run(xs[0], finish)
+    ys[0].finish()
     run(second[:2], ReduceRing.send_far)
-    compute(3)
-    run(sliced[0], begin)
-    run(sliced[3], forward)
-    run(sliced[1], finish)
+    batch(3, 0)
+    zs[1].forward_half(1)
+    xs[2][0].forward()
+    batch(3, 1)
+    xs[2][1].forward()
+    ys[2].forward()
+    run(xs[1], finish)
+    ys[1].finish()
     run(second[:2], ReduceRing.send_right)
-    deep.finish()
+    run(xs[3], forward)
+    ys[3].forward()
+    run(zs, finish)
     second[2].begin()
-    run(sliced[0], forward)
-    run(sliced[3], finish)
+    run(xs[2], finish)
+    ys[2].finish()
     run(second[:2], ReduceRing.send_left)
     whole_own.wait()
     whole_swap.wait()
@@ -499,7 +537,8 @@
             gp[h * HALF : (h + 1) * HALF, 0:HALF] += mm_nt(whole[h, x], whole[0, x])
             gp[h * HALF : (h + 1) * HALF, HALF:] += mm_nt(whole[h, x], whole[1, x])
     run(second, forward)
-    run(sliced[0], finish)
+    run(xs[3], finish)
+    ys[3].finish()
     for k in (2, 0, 1):
         second[k].finish()
         third[k].begin()

time: 219 us -> 210 us (0.959)
  Pallas kernels: 212 us -> 203 us
    pallas_call x1, Pallas kernels: 136 us -> 130 us  [reduce_terms(): pl.pallas_call(functools.partial(reduce_kernel, tuple(buffers)), out_shap...]
    pallas_call x1, Pallas kernels: 75.8 us -> 73.3 us  [gather(): pl.pallas_call(gather_kernel, out_shape=(jax.ShapeDtypeStruct((4, 4, 4, H...]
where the time goes in v5:
time: 210 us
  Pallas kernels  203 us (97%)
  local copies, waits for them, and re-layouts  4.29 us (2%)
    pallas_call x1, Pallas kernels, reduce_terms(): pl.pallas_call(functools.partial(reduce_kernel, tuple(buffers)), out_shap...  130 us
    pallas_call x1, Pallas kernels, gather(): pl.pallas_call(gather_kernel, out_shape=(jax.ShapeDtypeStruct((4, 4, 4, H...  73.3 us
  transfers between devices with their start and end apart: 1, of which 0 were waited for; matrix products, arithmetic and copies ran while one was open for 0% of the time, Pallas kernels for 35%

profile of v5, /device:TPU:1, one launch (start us, length us, event | category | flops | bytes accessed | tf_op | source)
XLA Modules:
  0.0 209.8 jit_solution(9520716039668360306)
XLA Ops:
  0.0 0.0 copy-start.1
  0.0 1.4 collective-permute-start
  1.4 73.3 %shard_map.37 = (bf16[4,4,4,128,1024]{4,3,2,1,0:T(8,128)(2,1)}, bf16[8,128,4096]{2,1,0:T(8,128)(2,1)}) custom-call(bf16[256,512]{1,0:T(8,128)(2,1)} %bitcast.23, bf16[8,128,4096]{2,1,0:T(8,128)(2,1)} %bitcast.20), custom_call_target="tpu_custom_call" | custom-call | tf_op jit(solution)/shard_map/pallas_call | solution.py:181
  74.7 0.0 collective-permute-done
  74.7 0.0 copy-done.1
  74.7 0.1 pad_add_fusion.1
  74.8 0.4 convert_reduce_fusion
  75.1 0.2 select_reduce_fusion.2
  75.3 0.0 copy-start
  75.3 0.5 copy-done
  75.9 0.1 copy.6
  75.9 0.6 reshape.94.slot_ref
  76.5 130.1 %shard_map.38 = bf16[256,4096]{1,0:T(8,128)(2,1)} custom-call(s32[16]{0:T(128)} %copy-done, s32[64]{0:T(128)} %reshape.94.slot_ref, bf16[8,128,4096]{2,1,0:T(8,128)(2,1)} %bitcast.21, bf16[8,128,4096]{2,1,0:T(8,128)(2,1)} %get-tuple-element.7.other_ref, bf16[4,4,4,128,1024]{4,3,2,1,0:T(8,128)(2,1)} %get-tuple-element.8.basis_ref, bf16[256,512]{1,0:T(8,128)(2,1)} %bitcast.24), custom_call_target="tpu_custom_call" | custom-call | tf_op jit(solution)/shard_map/pallas_call | solution.py:675
  206.6 3.1 %copy.8 = bf16[1,256,4096]{2,1,0:T(8,128)(2,1)} copy(bf16[1,256,4096]{2,1,0:T(8,128)(2,1)} %bitcast.22) | data formatting | bytes 4194304
  (4 shorter events, 0.0 us)
Async XLA Ops:
  0.0 74.7 %copy-start.1 = (s32[8,1]{0,1:T(1,128)S(1)}, s32[8,1]{0,1:T(1,128)}, u32[]{:S(2)}) copy-start(s32[8,1]{0,1:T(1,128)} %param.4) | copy-start | bytes 100
  0.0 74.7 %collective-permute-start = (s32[8]{0:T(128)}, s32[8]{0:T(128)S(1)}, u32[]{:S(2)}, u32[]{:S(2)}) collective-permute-start(s32[8]{0:T(128)} %bitcast.26), channel_id=1, source_target_pairs={{0,16},{16,0},{32,48},{48,32},{64,80},{80,64},{96,112},{112,96},{1... | collective-permute-start | bytes 104 | tf_op jit(solution)/shard_map/ppermute | solution.py:690
  75.3 0.5 copy-start

commit v6 on v5

--- a/solution.py
+++ b/solution.py
@@ -327,7 +327,7 @@
     shapes["gfull"] = pltpu.VMEM((L, L), f32)
     for name, count in (
         ("send", REDUCE_COPIES), ("recv", REDUCE_COPIES), ("load", 5),
-        ("pair_send", 9), ("pair_recv", 9), ("x_send", 10), ("x_recv", 10),
+        ("pair_send", 9), ("pair_recv", 9), ("x_send", 12), ("x_recv", 12),
     ):
         shapes[name] = pltpu.SemaphoreType.DMA((count,))
     return shapes
@@ -516,6 +516,13 @@
     batch(3, 0)
     zs[1].forward_half(1)
     xs[2][0].forward()
+    whole_own.wait()
+    whole_swap.wait()
+    gp[...] = jnp.zeros_like(gp)
+    for x in range(4):
+        for h in range(2):
+            gp[h * HALF : (h + 1) * HALF, 0:HALF] += mm_nt(whole[h, x], whole[0, x])
+            gp[h * HALF : (h + 1) * HALF, HALF:] += mm_nt(whole[h, x], whole[1, x])
     batch(3, 1)
     xs[2][1].forward()
     ys[2].forward()
@@ -529,13 +536,6 @@
     run(xs[2], finish)
     ys[2].finish()
     run(second[:2], ReduceRing.send_left)
-    whole_own.wait()
-    whole_swap.wait()
-    gp[...] = jnp.zeros_like(gp)
-    for x in range(4):
-        for h in range(2):
-            gp[h * HALF : (h + 1) * HALF, 0:HALF] += mm_nt(whole[h, x], whole[0, x])
-            gp[h * HALF : (h + 1) * HALF, HALF:] += mm_nt(whole[h, x], whole[1, x])
     run(second, forward)
     run(xs[3], finish)
     ys[3].finish()
@@ -578,16 +578,18 @@
     swap.wait()
     gin[...] = gin[...] + gp[mine, :]
     quarter = HALF // 2
-    right = across(gin, gx.at[0], 0, 1)
-    left = across(gin, gx.at[1], 1, 3)
+    right = across(gin.at[0:quarter], gx.at[0, 0:quarter], 0, 1)
+    left = across(gin.at[quarter:HALF], gx.at[1, quarter:HALF], 1, 3)
+    right_rest = across(gin.at[quarter:HALF], gx.at[0, quarter:HALF], 10, 1)
+    left_rest = across(gin.at[0:quarter], gx.at[1, 0:quarter], 11, 3)
     right.wait_recv()
     on_right = across(gx.at[0, 0:quarter], gx.at[2, 0:quarter], 2, 1)
     left.wait_recv()
     on_left = across(gx.at[1, quarter:HALF], gx.at[2, quarter:HALF], 3, 3)
     for c in (right, left):
         c.wait_send()
-    on_right.wait()
-    on_left.wait()
+    for c in (right_rest, left_rest, on_right, on_left):
+        c.wait()
     gfull[mine, :] = (gin[...] + gx[2]) + (gx[0] + gx[1])
     swap = give(gfull.at[mine], gfull.at[mine], 2)
     swap.wait()

time: 210 us -> 209 us (level)
  no operation moved by 1% of the time
where the time goes in v6:
time: 209 us
  Pallas kernels  203 us (97%)
  local copies, waits for them, and re-layouts  4.29 us (2%)
    pallas_call x1, Pallas kernels, reduce_terms(): pl.pallas_call(functools.partial(reduce_kernel, tuple(buffers)), out_shap...  129 us
    pallas_call x1, Pallas kernels, gather(): pl.pallas_call(gather_kernel, out_shape=(jax.ShapeDtypeStruct((4, 4, 4, H...  73.3 us
  transfers between devices with their start and end apart: 1, of which 0 were waited for; matrix products, arithmetic and copies ran while one was open for 0% of the time, Pallas kernels for 35%

profile of v6, /device:TPU:1, one launch (start us, length us, event | category | flops | bytes accessed | tf_op | source)
XLA Modules:
  0.0 208.9 jit_solution(7348159510552266578)
XLA Ops:
  0.0 0.0 copy-start.1
  0.0 1.4 collective-permute-start
  1.4 73.3 %shard_map.37 = (bf16[4,4,4,128,1024]{4,3,2,1,0:T(8,128)(2,1)}, bf16[8,128,4096]{2,1,0:T(8,128)(2,1)}) custom-call(bf16[256,512]{1,0:T(8,128)(2,1)} %bitcast.23, bf16[8,128,4096]{2,1,0:T(8,128)(2,1)} %bitcast.20), custom_call_target="tpu_custom_call" | custom-call | tf_op jit(solution)/shard_map/pallas_call | solution.py:181
  74.7 0.0 collective-permute-done
  74.7 0.0 copy-done.1
  74.7 0.1 pad_add_fusion.1
  74.8 0.4 convert_reduce_fusion
  75.1 0.2 select_reduce_fusion.2
  75.3 0.0 copy-start
  75.3 0.5 copy-done
  75.9 0.1 copy.6
  75.9 0.6 reshape.94.slot_ref
  76.5 129.3 %shard_map.38 = bf16[256,4096]{1,0:T(8,128)(2,1)} custom-call(s32[16]{0:T(128)} %copy-done, s32[64]{0:T(128)} %reshape.94.slot_ref, bf16[8,128,4096]{2,1,0:T(8,128)(2,1)} %bitcast.21, bf16[8,128,4096]{2,1,0:T(8,128)(2,1)} %get-tuple-element.7.other_ref, bf16[4,4,4,128,1024]{4,3,2,1,0:T(8,128)(2,1)} %get-tuple-element.8.basis_ref, bf16[256,512]{1,0:T(8,128)(2,1)} %bitcast.24), custom_call_target="tpu_custom_call" | custom-call | tf_op jit(solution)/shard_map/pallas_call | solution.py:677
  205.8 3.1 %copy.8 = bf16[1,256,4096]{2,1,0:T(8,128)(2,1)} copy(bf16[1,256,4096]{2,1,0:T(8,128)(2,1)} %bitcast.22) | data formatting | bytes 4194304
  (4 shorter events, 0.0 us)
Async XLA Ops:
  0.0 74.7 %copy-start.1 = (s32[8,1]{0,1:T(1,128)S(1)}, s32[8,1]{0,1:T(1,128)}, u32[]{:S(2)}) copy-start(s32[8,1]{0,1:T(1,128)} %param.4) | copy-start | bytes 100
  0.0 74.7 %collective-permute-start = (s32[8]{0:T(128)}, s32[8]{0:T(128)S(1)}, u32[]{:S(2)}, u32[]{:S(2)}) collective-permute-start(s32[8]{0:T(128)} %bitcast.26), channel_id=1, source_target_pairs={{0,16},{16,0},{32,48},{48,32},{64,80},{80,64},{96,112},{112,96},{1... | collective-permute-start | bytes 104 | tf_op jit(solution)/shard_map/ppermute | solution.py:692
  75.3 0.5 copy-start
